TPU v7x, 128 devices: a whole 4x4x4 slice. The times are simulated.
128 devices in a mesh: dim: 16 (over y, x), batch: 8 (over z, core).
Axes of the slice: x: 4, y: 4, z: 4, core: 2. Of those that a mesh axis runs over, the one named last changes fastest.
Arguments:
- start: float32 [2048, 4096], P('batch', 'dim'), may hold values from -6 to 6
- increments: float32 [3, 2048, 4096], P(None, 'batch', 'dim'), may hold values from -0.75 to 0.75
- w_in: bfloat16 [4096, 4096], P(None, 'dim'), may hold values from -0.09375 to 0.09375
- w_out: bfloat16 [4096, 4096], P('dim'), may hold values from -0.09375 to 0.09375
- initial: float32 [], replicated, may hold values from 4 to 5.5
Outputs:
- residual: float32 [2048], P('batch')
- grad_in: float32 [4096, 4096], P('batch', 'dim')
- grad_out: float32 [4096, 4096], P('dim', 'batch')
All inputs are finite; a program needn't handle non-finite values.
Results may differ from a plain program's by a relative error of at most 0.0051.
Values may be sent and summed in bfloat16 or wider, within the bound.
A program may use at most 128 MiB of HBM per device.

v0:
```python
import math

import jax
import jax.numpy as jnp
from jax import lax
from jax.sharding import Mesh
from jax.sharding import PartitionSpec as P

D = 4096
STEPS = 3
DIM = ("dim_0", "dim_1")


time_step = 1.0 / 64.0
lam_coef = 50.0
noise_coef = math.sqrt(2.0)


def from_everyone(array, axis):
    copies = jnp.broadcast_to(array, (lax.axis_size(axis), *array.shape))
    return lax.all_to_all(copies, axis, split_axis=0, concat_axis=0, tiled=True)


def in_order(blocks, dim):
    blocks = jnp.moveaxis(blocks, 0, dim)
    shape = blocks.shape
    return blocks.reshape(*shape[:dim], shape[dim] * shape[dim + 1], *shape[dim + 2 :])


def gathered_copies(array, axis, dim):
    blocks = from_everyone(array, axis)
    return in_order(blocks, dim)


def gathered_by_axis(array, axes, dim):
    whole = array
    for number in range(len(axes) - 1, -1, -1):
        whole = lax.all_gather(whole, axes[number], axis=dim, tiled=True)
    return whole


def one_axis_at_a_time(array, axes):
    for axis in axes:
        array = lax.psum(array, axis)
    return array


def cut_along(array, dim, devices):
    before, after = (array.shape[:dim], array.shape[dim + 1 :])
    return jnp.moveaxis(array.reshape(*before, devices, -1, *after), dim, 0)


def sum_together(arrays, axis, dims):
    devices = lax.axis_size(axis)
    blocks = [cut_along(a, dim, devices) for a, dim in zip(arrays, dims)]
    lines = jnp.concatenate([b.reshape(devices, -1) for b in blocks], axis=1)
    extent = max(16, -(-lines.shape[1] // 1024) * 8)
    lines = jnp.pad(lines, ((0, 0), (0, extent * 128 - lines.shape[1]))).reshape(-1, 128)
    vector, at, done = (lax.psum_scatter(lines, axis, tiled=True).reshape(-1), 0, [])
    for b in blocks:
        part = b[0]
        done.append(vector[at : at + part.size].reshape(part.shape))
        at += part.size
    return tuple(done)


def on_device(start, increments, w_in, w_out, initial):
    zscale = 2.0 / math.sqrt(D)
    state = start
    saved = []
    local_total = jnp.zeros((start.shape[0],), jnp.float32)
    out_cols = lax.all_to_all(w_out, DIM, split_axis=1, concat_axis=0, tiled=True)
    for step in range(STEPS):
        inc = increments[step]
        whole = gathered_copies(state.astype(jnp.bfloat16), DIM, 1)
        hidden = jnp.dot(whole, w_in, preferred_element_type=jnp.float32)
        act = jax.nn.silu(hidden).astype(jnp.bfloat16)
        act_whole = gathered_by_axis(act, DIM, 1)
        zval = zscale * jnp.dot(act_whole, out_cols, preferred_element_type=jnp.float32)
        inner = jnp.sum(zval * inc, 1)
        square = jnp.sum(zval * zval, 1)
        local_total = local_total + 0.5 * lam_coef * time_step * square + inner
        saved.append((whole, hidden, act, zval))
        state = state + noise_coef * inc
    norm_local = jnp.sum(state * state, 1)
    ysum, norm_sq = (one_axis_at_a_time(local_total, DIM), one_axis_at_a_time(norm_local, DIM))
    residual = initial + ysum - jnp.log((1.0 + norm_sq) * 0.5)
    grad_in = jnp.zeros(w_in.shape, jnp.float32)
    grad_out = jnp.zeros(w_out.shape, jnp.float32)
    reduced_in = None
    reduced_out = None
    for step in range(STEPS):
        whole, hidden, act, zval = saved[step]
        gz = (zscale * residual[:, None] * (lam_coef * time_step * zval + increments[step])).astype(
            jnp.bfloat16
        )
        gz_whole = gathered_copies(gz, DIM, 1)
        term_out = jnp.dot(act.T, gz_whole, preferred_element_type=jnp.float32)
        ga = jnp.dot(gz_whole, w_out.T, preferred_element_type=jnp.float32)
        sig = jax.nn.sigmoid(hidden)
        gh = (ga * sig * (1.0 + hidden * (1.0 - sig))).astype(jnp.bfloat16)
        term_in = jnp.dot(whole.T, gh, preferred_element_type=jnp.float32)
        grad_in = grad_in + term_in
        grad_out = grad_out + term_out
    reduced_in, reduced_out = sum_together((grad_in, grad_out), "batch", (0, 1))
    return (residual, reduced_in, reduced_out)


def solution(mesh):
    finer = Mesh(mesh.devices.reshape(4, 4, mesh.shape["batch"]), ("dim_0", "dim_1", "batch"))
    return jax.shard_map(
        on_device,
        mesh=finer,
        in_specs=(P("batch", DIM), P(None, "batch", DIM), P(None, DIM), P(DIM, None), P()),
        out_specs=(P("batch"), P("batch", DIM), P(DIM, "batch")),
        check_vma=False,
    )
```

profile of v0, /device:TPU:1, one launch (start us, length us, event | category | flops | bytes accessed | tf_op | source)
XLA Modules:
  0.0 411.1 jit_solution(700300578174135551)
XLA Ops:
  10.0 34.6 %all_to_all.49 = bf16[16,256,256]{1,2,0:T(8,128)(2,1)S(1)} all-to-all(bf16[16,256,256]{1,2,0:T(8,128)(2,1)S(1)} %broadcast_in_dim.22), channel_id=1, replica_groups=mesh['dim_0'=4,'dim_1'=4,'batch'=8] {'dim_0','dim_1'}, dimensions={0} | all-to-all | bytes 4194304 | tf_op jit(solution)/shard_map/all_to_all | solution.py:21
  46.1 10.9 %all_gather.20 = bf16[256,1024]{1,0:T(8,128)(2,1)} all-gather(bf16[256,256]{1,0:T(8,128)(2,1)S(1)} %get-tuple-element.28), channel_id=1, replica_groups=mesh['dim_0'=4,'dim_1'=4,'batch'=8] {'dim_1'}, dimensions={1}, use_global_device_ids=true | all-gather | bytes 655360 | tf_op jit(solution)/shard_map/all_gather | solution.py:38
  57.3 28.2 %all_to_all.50 = bf16[16,256,256]{1,2,0:T(8,128)(2,1)S(1)} all-to-all(bf16[16,256,256]{1,2,0:T(8,128)(2,1)S(1)} %broadcast_in_dim.23), channel_id=1, replica_groups=mesh['dim_0'=4,'dim_1'=4,'batch'=8] {'dim_0','dim_1'}, dimensions={0} | all-to-all | bytes 4194304 | tf_op jit(solution)/shard_map/all_to_all | solution.py:21
  86.9 14.8 %all_gather.22 = bf16[256,1024]{1,0:T(8,128)(2,1)} all-gather(bf16[256,256]{1,0:T(8,128)(2,1)S(1)} %get-tuple-element.30), channel_id=1, replica_groups=mesh['dim_0'=4,'dim_1'=4,'batch'=8] {'dim_1'}, dimensions={1}, use_global_device_ids=true | all-gather | bytes 655360 | tf_op jit(solution)/shard_map/all_gather | solution.py:38
  102.1 25.2 %all_to_all.51 = bf16[16,256,256]{1,2,0:T(8,128)(2,1)S(1)} all-to-all(bf16[16,256,256]{1,2,0:T(8,128)(2,1)S(1)} %broadcast_in_dim.21), channel_id=1, replica_groups=mesh['dim_0'=4,'dim_1'=4,'batch'=8] {'dim_0','dim_1'}, dimensions={0} | all-to-all | bytes 4194304 | tf_op jit(solution)/shard_map/all_to_all | solution.py:21
  128.8 11.6 %all_gather.18 = bf16[256,1024]{1,0:T(8,128)(2,1)} all-gather(bf16[256,256]{1,0:T(8,128)(2,1)S(1)} %get-tuple-element.26), channel_id=1, replica_groups=mesh['dim_0'=4,'dim_1'=4,'batch'=8] {'dim_1'}, dimensions={1}, use_global_device_ids=true | all-gather | bytes 655360 | tf_op jit(solution)/shard_map/all_gather | solution.py:38
  140.4 4.1 %copy.28 = bf16[256,4096]{0,1:T(8,128)(2,1)} copy(bf16[256,4096]{1,0:T(8,128)(2,1)} %param.8) | data formatting | bytes 4194304 | tf_op args[3]
  144.5 4.2 %all-to-all-start.1 = ((bf16[256,16,256]{0,2,1:T(8,128)(2,1)}), bf16[256,16,256]{0,2,1:T(8,128)(2,1)S(1)}, u32[]{:S(2)}, u32[]{:S(2)}) async-start(bf16[256,16,256]{0,2,1:T(8,128)(2,1)} %bitcast.122), calls=%async_computation.1 | async-start | bytes 4194304 | tf_op jit(solution)/shard_map/all_to_all | solution.py:72
  149.5 19.0 %all-to-all-done.1 = bf16[256,16,256]{0,2,1:T(8,128)(2,1)S(1)} async-done(((bf16[256,16,256]{0,2,1:T(8,128)(2,1)}), bf16[256,16,256]{0,2,1:T(8,128)(2,1)S(1)}, u32[]{:S(2)}, u32[]{:S(2)}) %all-to-all-start.1) | async-done | bytes 2097184 | tf_op jit(solution)/shard_map/all_to_all | solution.py:72
  169.9 2.8 copy.29
  172.8 2.5 fusion.39
  175.3 2.5 fusion.40
  177.8 19.8 %all-gather.4.cloned.1.call-done = bf16[256,4096]{1,0:T(8,128)(2,1)} async-done(((bf16[256,1024]{1,0:T(8,128)(2,1)}), bf16[256,4096]{1,0:T(8,128)(2,1)}) %all-gather.4.cloned.1.call-update) | async-done | bytes 2097168 | tf_op jit(solution)/shard_map/all_gather | solution.py:38
  197.6 3.3 multiply_reduce_fusion.2
  200.9 6.6 %all-reduce.1 = (f32[256]{0:T(256)S(1)}, f32[256]{0:T(256)S(1)}) all-reduce(f32[256]{0:T(256)S(1)} %get-tuple-element.5, f32[256]{0:T(256)S(1)} %add_add_fusion), channel_id=1, replica_groups=mesh['dim_0'=4,'dim_1'=4,'batch'=8] {'dim_0'}, use_global_device_ids=true, to_apply=%region_9.10 | all-reduce | flops 512 | bytes 4096 | tf_op jit(solution)/shard_map/psum | solution.py:44
  207.5 8.3 %all-reduce = (f32[256]{0:T(256)S(1)}, f32[256]{0:T(256)S(1)}) all-reduce(f32[256]{0:T(256)S(1)} %get-tuple-element.12, f32[256]{0:T(256)S(1)} %get-tuple-element.13), channel_id=1, replica_groups=mesh['dim_0'=4,'dim_1'=4,'batch'=8] {'dim_1'}, use_global_device_ids=true, to_apply=%region_10.11 | all-reduce | flops 512 | bytes 4096 | tf_op jit(solution)/shard_map/psum | solution.py:44
  217.7 27.4 %all_to_all.52 = bf16[16,256,256]{1,2,0:T(8,128)(2,1)} all-to-all(bf16[16,256,256]{1,2,0:T(8,128)(2,1)S(1)} %broadcast_in_dim.24), channel_id=1, replica_groups=mesh['dim_0'=4,'dim_1'=4,'batch'=8] {'dim_0','dim_1'}, dimensions={0} | all-to-all | bytes 4194304 | tf_op jit(solution)/shard_map/all_to_all | solution.py:21
  245.3 26.5 %all_to_all.53 = bf16[16,256,256]{1,2,0:T(8,128)(2,1)} all-to-all(bf16[16,256,256]{1,2,0:T(8,128)(2,1)S(1)} %broadcast_in_dim.25), channel_id=1, replica_groups=mesh['dim_0'=4,'dim_1'=4,'batch'=8] {'dim_0','dim_1'}, dimensions={0} | all-to-all | bytes 4194304 | tf_op jit(solution)/shard_map/all_to_all | solution.py:21
  273.4 4.4 %all-to-all-start.6 = ((bf16[16,256,256]{1,2,0:T(8,128)(2,1)}), bf16[16,256,256]{1,2,0:T(8,128)(2,1)}, u32[]{:S(2)}, u32[]{:S(2)}) async-start(bf16[16,256,256]{1,2,0:T(8,128)(2,1)} %broadcast_in_dim.26), calls=%async_computation.6 | async-start | bytes 4194304 | tf_op jit(solution)/shard_map/all_to_all | solution.py:21
  278.1 4.5 %fusion.41 = f32[256,4096]{1,0:T(8,128)} fusion(bf16[256,256]{1,0:T(8,128)(2,1)S(1)} %get-tuple-element.26, bf16[256,4096]{0,1:T(8,128)(2,1)} %bitcast.113), kind=kOutput, calls=%fused_computation.71 | convolution fusion | flops 536870912 | bytes 6422528 | tf_op jit(solution)/shard_map/dot_general | solution.py:98
  282.5 6.8 %convolution_bitcast_fusion = f32[4096,256]{0,1:T(8,128)} fusion(bf16[256,4096]{0,1:T(8,128)(2,1)} %bitcast.124, bf16[256,4096]{0,1:T(8,128)(2,1)} %bitcast.114, bf16[256,4096]{1,0:T(8,128)(2,1)S(1)} %copy-done.2, f32[256,256]{1,0:T(8,128)S(1)} %copy-done.18), kind=kOutput, calls=%fused_computation.5 | convolution fusion | flops 1074331648 | bytes 10747904 | tf_op jit(solution)/shard_map/dot_general | solution.py:102
  289.3 8.0 %convolution_add_fusion.3 = f32[4096,256]{0,1:T(8,128)} fusion(f32[4096,256]{0,1:T(8,128)} %convolution_bitcast_fusion, bf16[256,4096]{0,1:T(8,128)(2,1)} %bitcast.118, bf16[256,4096]{0,1:T(8,128)(2,1)} %bitcast.111, bf16[256,4096]{1,0:T(8,128)(2,1)S(1)} %copy-done.2, f32[256,256]{1,0:T(8,128)S(1)} %copy-done.16), kind=kOutput, calls=%fused_computation.4 | convolution fusion | flops 1075380224 | bytes 14942208 | tf_op jit(solution)/shard_map/dot_general | solution.py:102
  297.3 4.3 %all-to-all-done.6 = bf16[16,256,256]{1,2,0:T(8,128)(2,1)} async-done(((bf16[16,256,256]{1,2,0:T(8,128)(2,1)}), bf16[16,256,256]{1,2,0:T(8,128)(2,1)}, u32[]{:S(2)}, u32[]{:S(2)}) %all-to-all-start.6) | async-done | bytes 2097184 | tf_op jit(solution)/shard_map/all_to_all | solution.py:21
  301.5 7.9 %convolution_add_fusion.2 = f32[4096,256]{0,1:T(8,128)} fusion(f32[4096,256]{0,1:T(8,128)} %convolution_add_fusion.3, bf16[256,4096]{0,1:T(8,128)(2,1)} %bitcast.120, bf16[256,4096]{0,1:T(8,128)(2,1)} %bitcast.21, bf16[256,4096]{1,0:T(8,128)(2,1)S(1)} %copy-done.2, f32[256,256]{1,0:T(8,128)S(1)} %copy-done.17), kind=kOutput, calls=%fused_computation.3 | convolution fusion | flops 1075380224 | bytes 14942208 | tf_op jit(solution)/shard_map/dot_general | solution.py:102
  309.5 5.6 %copy.36 = f32[4096,256]{1,0:T(8,128)} copy(f32[4096,256]{0,1:T(8,128)} %convolution_add_fusion.2) | data formatting | bytes 8388608 | tf_op jit(solution)/shard_map/add | solution.py:103
  315.1 5.1 %reshape_reshape.3 = f32[8,131072]{1,0:T(8,128)} reshape(f32[4096,256]{1,0:T(8,128)} %copy.36) | data formatting | bytes 8388608 | tf_op jit(solution)/shard_map/reshape;reshape | solution.py:56
  320.2 3.0 convolution_add_fusion.1
  323.2 2.4 convolution_add_fusion
  325.6 3.9 copy.42
  329.5 6.8 %pad_maximum_fusion = f32[8,262144]{1,0:T(8,128)} fusion(f32[8,131072]{1,0:T(8,128)S(1)} %bitcast.116, f32[8,131072]{1,0:T(8,128)S(1)} %copy-done.4), kind=kLoop, calls=%fused_computation | loop fusion | flops 2097152 | bytes 16777216 | tf_op jit(solution)/shard_map/concatenate | solution.py:56
  336.3 7.8 %reshape.57 = f32[16384,128]{1,0:T(8,128)} reshape(f32[8,262144]{1,0:T(8,128)} %pad_maximum_fusion) | data formatting | bytes 16777216 | tf_op jit(solution)/shard_map/reshape | solution.py:58
  344.2 57.3 %reduce-scatter.2.cloned.1.call-done = f32[2048,128]{1,0:T(8,128)} async-done(((f32[16384,128]{1,0:T(8,128)}), f32[2048,128]{1,0:T(8,128)}) %reduce-scatter.2.cloned.1.call-update) | async-done | bytes 1048592 | tf_op jit(solution)/shard_map/reduce_scatter | solution.py:59
  (71 shorter events, 16.2 us)
Async XLA Ops:
  7.2 37.5 %copy-start = (bf16[4096,256]{1,0:T(8,128)(2,1)S(1)}, bf16[4096,256]{1,0:T(8,128)(2,1)}, u32[]{:S(2)}) copy-start(bf16[4096,256]{1,0:T(8,128)(2,1)} %param.7) | copy-start | bytes 6291460
  7.2 2.4 copy-start.10
  7.2 165.6 %all-gather.6.cloned.1.call-start = ((), (), s32[]{:S(2)}) async-start(), calls=%async_computation.9 | async-start | bytes 2621440 | tf_op jit(solution)/shard_map/all_gather | solution.py:38
  9.7 34.9 %copy-start.9 = (f32[256,256]{0,1:T(8,128)}, f32[256,256]{0,1:T(8,128)S(1)}, u32[]{:S(2)}) copy-start(f32[256,256]{0,1:T(8,128)S(1)} %copy.31) | copy-start | bytes 786436
  44.6 1.4 copy-start.5
  46.1 39.3 %copy-start.12 = (bf16[256,256]{1,0:T(8,128)(2,1)}, bf16[256,256]{1,0:T(8,128)(2,1)S(1)}, u32[]{:S(2)}) copy-start(bf16[256,256]{1,0:T(8,128)(2,1)S(1)} %get-tuple-element.28) | copy-start | bytes 393220
  57.0 118.3 %all-gather.8.cloned.1.call-start = ((), (), s32[]{:S(2)}) async-start(), calls=%async_computation.10 | async-start | bytes 2621440 | tf_op jit(solution)/shard_map/all_gather | solution.py:38
  85.4 1.5 copy-start.6
  86.9 14.9 %copy-start.14 = (bf16[256,256]{1,0:T(8,128)(2,1)}, bf16[256,256]{1,0:T(8,128)(2,1)S(1)}, u32[]{:S(2)}) copy-start(bf16[256,256]{1,0:T(8,128)(2,1)S(1)} %get-tuple-element.30) | copy-start | bytes 393220
  101.7 95.9 %all-gather.4.cloned.1.call-start = ((), (), s32[]{:S(2)}) async-start(), calls=%async_computation.8 | async-start | bytes 2621440 | tf_op jit(solution)/shard_map/all_gather | solution.py:38
  127.3 1.5 copy-start.8
  144.5 4.2 %copy-start.11 = (f32[1,256,256]{2,1,0:T(8,128)S(1)}, f32[1,256,256]{2,1,0:T(8,128)}, u32[]{:S(2)}) copy-start(f32[1,256,256]{2,1,0:T(8,128)} %get-tuple-element.20) | copy-start | bytes 786436
  144.5 24.0 %all-to-all-start.1 = ((bf16[256,16,256]{0,2,1:T(8,128)(2,1)}), bf16[256,16,256]{0,2,1:T(8,128)(2,1)S(1)}, u32[]{:S(2)}, u32[]{:S(2)}) async-start(bf16[256,16,256]{0,2,1:T(8,128)(2,1)} %bitcast.122), calls=%async_computation.1 | async-start | bytes 4194304 | tf_op jit(solution)/shard_map/all_to_all | solution.py:72
  168.5 1.3 copy-start.7
  273.4 28.2 %all-to-all-start.6 = ((bf16[16,256,256]{1,2,0:T(8,128)(2,1)}), bf16[16,256,256]{1,2,0:T(8,128)(2,1)}, u32[]{:S(2)}, u32[]{:S(2)}) async-start(bf16[16,256,256]{1,2,0:T(8,128)(2,1)} %broadcast_in_dim.26), calls=%async_computation.6 | async-start | bytes 4194304 | tf_op jit(solution)/shard_map/all_to_all | solution.py:21
  277.8 123.7 %reduce-scatter.2.cloned.1.call-start = ((), (), s32[]{:S(2)}) async-start(), calls=%async_computation.11 | async-start | bytes 9437184 | tf_op jit(solution)/shard_map/reduce_scatter | solution.py:59
  278.0 4.5 %copy-start.2 = (bf16[256,4096]{1,0:T(8,128)(2,1)S(1)}, bf16[256,4096]{1,0:T(8,128)(2,1)}, u32[]{:S(2)}) copy-start(bf16[256,4096]{1,0:T(8,128)(2,1)} %param.8) | copy-start | bytes 6291460
  278.1 4.5 %copy-start.18 = (f32[256,256]{1,0:T(8,128)S(1)}, f32[256,256]{1,0:T(8,128)}, u32[]{:S(2)}) copy-start(f32[256,256]{1,0:T(8,128)} %get-tuple-element.27) | copy-start | bytes 786436
  282.5 6.8 %copy-start.16 = (f32[256,256]{1,0:T(8,128)S(1)}, f32[256,256]{1,0:T(8,128)}, u32[]{:S(2)}) copy-start(f32[256,256]{1,0:T(8,128)} %get-tuple-element.29) | copy-start | bytes 786436
  289.3 12.2 %copy-start.17 = (f32[256,256]{1,0:T(8,128)S(1)}, f32[256,256]{1,0:T(8,128)}, u32[]{:S(2)}) copy-start(f32[256,256]{1,0:T(8,128)} %get-tuple-element.31) | copy-start | bytes 786436
  315.1 5.1 %copy-start.3 = (bf16[16,256,256]{1,2,0:T(8,128)(2,1)S(1)}, bf16[16,256,256]{1,2,0:T(8,128)(2,1)}, u32[]{:S(2)}) copy-start(bf16[16,256,256]{1,2,0:T(8,128)(2,1)} %all_to_all.53) | copy-start | bytes 6291460
  315.1 5.1 %copy-start.13 = (bf16[256,256]{1,0:T(8,128)(2,1)S(1)}, bf16[256,256]{1,0:T(8,128)(2,1)}, u32[]{:S(2)}) copy-start(bf16[256,256]{1,0:T(8,128)(2,1)} %copy-done.12) | copy-start | bytes 393220
  320.2 3.0 copy-start.15
  325.6 3.9 copy-start.4
  344.2 60.4 %copy-start.1 = (bf16[4096,256]{1,0:T(8,128)(2,1)S(1)}, bf16[4096,256]{1,0:T(8,128)(2,1)}, u32[]{:S(2)}) copy-start(bf16[4096,256]{1,0:T(8,128)(2,1)} %param.7) | copy-start | bytes 6291460
Sparse Core Ops, SparseCore 0:
  57.1 47.8 all-gather.5
  106.7 43.1 all-gather.7
  151.5 46.0 all-gather.3
  344.3 57.1 reduce-scatter.1
where the time goes:
time: 412 us; the launch traced here: 411 us
  blocking collectives  194 us (47%)
  waiting for transfers between devices  100 us (24%)
  matrix products  45.2 us (11%)
  local copies, waits for them, and re-layouts  39 us (9%)
  between operations  14.7 us (4%)
  starting transfers between devices  8.96 us (2%)
  other arithmetic  8.55 us (2%)
    all_to_all x5, blocking collectives, from_everyone(): return lax.all_to_all(copies, axis, split_axis=0, concat_axis=0, tiled=True)  142 us
    reduce_scatter x1, waiting for transfers between devices, sum_together(): lax.psum_scatter(lines, axis, tiled=True).reshape(-1)  57.3 us
    all_gather x3, blocking collectives, gathered_by_axis(): whole = lax.all_gather(whole, axes[number], axis=dim, tiled=True)  37.3 us
    dot_general x3, matrix products, on_device(): term_in = jnp.dot(whole.T, gh, preferred_element_type=jnp.float32)  22.7 us
    all_gather x3, waiting for transfers between devices, gathered_by_axis(): whole = lax.all_gather(whole, axes[number], axis=dim, tiled=True)  19.8 us
    all_to_all x1, waiting for transfers between devices, on_device(): lax.all_to_all(w_out, DIM, split_axis=1, concat_axis=0, tiled=True)  19 us
    psum x2, blocking collectives, one_axis_at_a_time(): array = lax.psum(array, axis)  14.9 us
    unnamed x44, local copies, waits for them, and re-layouts  9.91 us
  transfers between devices with their start and end apart: 6, of which 4 were waited for; matrix products, arithmetic and copies ran while one was open for 8% of the time, Pallas kernels for 0%

commit v1 on v0

v1 whole, which is shorter than its diff:
```python
import math

import jax
import jax.numpy as jnp
from jax import lax
from jax.sharding import Mesh
from jax.sharding import PartitionSpec as P

D = 4096
STEPS = 3
DIM = ("y", "x")
BATCH = ("z", "c")

time_step = 1.0 / 64.0
lam_coef = 50.0
noise_coef = math.sqrt(2.0)


def a2a(array, axis):
    return lax.all_to_all(array, axis, split_axis=0, concat_axis=0, tiled=True)


def scatter_sum(parts, axis):
    got = a2a(parts.astype(jnp.bfloat16), axis)
    return jnp.sum(got.astype(jnp.float32), 0)


def on_device(start, increments, w_in, w_out, initial):
    zscale = 2.0 / math.sqrt(D)
    rows, width = start.shape
    f32, bf16 = jnp.float32, jnp.bfloat16
    win = a2a(w_in.reshape(4, 4, width, width).transpose(1, 0, 2, 3), "x")
    wout = a2a(w_out.reshape(width, 4, 4, width).transpose(2, 1, 0, 3), "x")
    states = [start]
    for step in range(STEPS):
        states.append(states[-1] + noise_coef * increments[step])
    xb = jnp.stack(states[:STEPS]).astype(bf16).reshape(STEPS * rows, width)
    inc = increments.reshape(STEPS * rows, width)
    xg = lax.all_gather(xb, "y")
    h = scatter_sum(jnp.einsum("jrd,ijdh->irh", xg, win, preferred_element_type=f32), "x")
    act = jax.nn.silu(h).astype(bf16)
    ag = lax.all_gather(act, "x")
    z = zscale * scatter_sum(jnp.einsum("irh,ijhd->jrd", ag, wout, preferred_element_type=f32), "y")
    terms = jnp.sum((0.5 * lam_coef * time_step * z * z + z * inc).reshape(STEPS, rows, width), (0, 2))
    norm = jnp.sum(states[STEPS] * states[STEPS], 1)
    both = lax.psum(jnp.stack([terms, norm]), DIM)
    residual = initial + both[0] - jnp.log((1.0 + both[1]) * 0.5)
    scale = jnp.tile(zscale * residual, STEPS)[:, None]
    gz = (scale * (lam_coef * time_step * z + inc)).astype(bf16)
    gg = lax.all_gather(gz, "y")
    ga = scatter_sum(jnp.einsum("jrd,ijhd->irh", gg, wout, preferred_element_type=f32), "x")
    sig = jax.nn.sigmoid(h)
    gh = (ga * sig * (1.0 + h * (1.0 - sig))).astype(bf16)
    hg = lax.all_gather(gh, "x")
    gout = jnp.einsum("irh,jrd->jihd", ag, gg, preferred_element_type=f32)
    gin = jnp.einsum("jrd,irh->jidh", xg, hg, preferred_element_type=f32)
    grads = jnp.stack([gin, gout], 1)
    grads = grads.reshape(4, 2, 2, 2, width, width).transpose(3, 0, 1, 2, 4, 5)
    grads = lax.psum_scatter(grads.reshape(2, 4, -1), "c", scatter_dimension=0, tiled=False)
    grads = scatter_sum(grads, "z").reshape(2, 2, width, width)
    grads = lax.all_gather(grads, "c")
    grads = grads.transpose(2, 0, 1, 3, 4).reshape(4, -1)
    grads = a2a(grads.astype(bf16), "x").astype(f32).reshape(2, 2, 2, width, width)
    mine = lax.dynamic_index_in_dim(grads, lax.axis_index("c"), 0, keepdims=False)
    return residual, mine[:, 0].reshape(2 * width, width), mine[:, 1].transpose(1, 0, 2).reshape(width, 2 * width)


def solution(mesh):
    finer = Mesh(mesh.devices.reshape(4, 4, 4, 2), ("y", "x", "z", "c"))
    return jax.shard_map(
        on_device,
        mesh=finer,
        in_specs=(P(BATCH, DIM), P(None, BATCH, DIM), P(None, DIM), P(DIM, None), P()),
        out_specs=(P(BATCH), P(BATCH, DIM), P(DIM, BATCH)),
        check_vma=False,
    )
```

time: 412 us -> 440 us (1.068); the launches traced: 411 us -> 433 us
  other arithmetic: 8.55 us -> 46.3 us
  matrix products: 45.2 us -> 22.5 us
  blocking collectives: 194 us -> 203 us
  waiting for transfers between devices: 100 us -> 92.5 us
  local copies, waits for them, and re-layouts: 39 us -> 45.3 us
    reduce_scatter x1 -> x0, waiting for transfers between devices: 57.3 us -> none  [sum_together(): lax.psum_scatter(lines, axis, tiled=True).reshape(-1)]
    all_gather x3 -> x5, waiting for transfers between devices: 19.8 us -> 58.5 us  [the longest x1 31.8 us: on_device(): gg = lax.all_gather(gz, 'y')]
    all_gather x3 -> x0, blocking collectives: 37.3 us -> none  [gathered_by_axis(): whole = lax.all_gather(whole, axes[number], axis=dim, tiled=True)]
    unnamed x0 -> x1, blocking collectives: none -> 26.2 us
    dot_general x12 -> x5, matrix products: 45.2 us -> 22.5 us  [the longest x1 5.16 us: on_device(): gin = jnp.einsum('jrd,irh->jidh', xg, hg, preferred_element_type=f32)]
    convert_element_type x3 -> x6, other arithmetic: 1.14 us -> 21.4 us  [the longest x1 7.44 us: on_device(): grads.astype(bf16)]
    reduce_sum x0 -> x5, other arithmetic: none -> 14.3 us  [the longest x4 14.1 us: scatter_sum(): return jnp.sum(got.astype(jnp.float32), 0)]
    psum x2 -> x1, blocking collectives: 14.9 us -> 28.5 us  [on_device(): both = lax.psum(jnp.stack([terms, norm]), DIM)]
  transfers between devices with their start and end apart: 6 -> 7, of which waited for: 4 -> 6; matrix products, arithmetic and copies ran while one was open for 8% -> 4% of each run, Pallas kernels for 0% -> 0%
where the time goes in v1:
time: 440 us; the launch traced here: 433 us
  blocking collectives  203 us (46%)
  waiting for transfers between devices  92.5 us (21%)
  other arithmetic  46.3 us (11%)
  local copies, waits for them, and re-layouts  45.3 us (10%)
  matrix products  22.5 us (5%)
  between operations  15.1 us (3%)
  starting transfers between devices  9.04 us (2%)
    all_to_all x5, blocking collectives, a2a(): return lax.all_to_all(array, axis, split_axis=0, concat_axis=0, tiled=True)  148 us
    all_to_all x2, waiting for transfers between devices, a2a(): return lax.all_to_all(array, axis, split_axis=0, concat_axis=0, tiled=True)  33.9 us
    all_gather x1, waiting for transfers between devices, on_device(): gg = lax.all_gather(gz, 'y')  31.8 us
    psum x1, blocking collectives, on_device(): both = lax.psum(jnp.stack([terms, norm]), DIM)  28.5 us
    unnamed x1, blocking collectives  26.2 us
    unnamed x20, local copies, waits for them, and re-layouts  16.3 us
    all_gather x1, waiting for transfers between devices, on_device(): hg = lax.all_gather(gh, 'x')  14.2 us
    reduce_sum x4, other arithmetic, scatter_sum(): return jnp.sum(got.astype(jnp.float32), 0)  14.1 us
  transfers between devices with their start and end apart: 7, of which 6 were waited for; matrix products, arithmetic and copies ran while one was open for 4% of the time, Pallas kernels for 0%

profile of v1, /device:TPU:1, one launch (start us, length us, event | category | flops | bytes accessed | tf_op | source)
XLA Modules:
  0.0 433.3 jit_solution(6734123639831771158)
XLA Ops:
  9.8 30.1 %all_to_all.37 = bf16[4,4,256,256]{3,2,1,0:T(8,128)(2,1)S(1)} all-to-all(bf16[4,4,256,256]{3,2,1,0:T(8,128)(2,1)S(1)} %bitcast.164), channel_id=1, replica_groups=mesh['y'=4,'x'=4,'z'=4,'c'=2] {'x'}, dimensions={0} | all-to-all | bytes 4194304 | tf_op jit(solution)/shard_map/all_to_all | solution.py:20
  39.9 3.2 fusion.10
  43.1 23.3 %all_to_all.38 = bf16[4,768,256]{2,1,0:T(8,128)(2,1)S(1)} all-to-all(bf16[4,768,256]{2,1,0:T(8,128)(2,1)S(1)} %fusion.10), channel_id=1, replica_groups=mesh['y'=4,'x'=4,'z'=4,'c'=2] {'x'}, dimensions={0} | all-to-all | bytes 3145728 | tf_op jit(solution)/shard_map/all_to_all | solution.py:20
  68.1 2.5 copy.43
  70.6 2.8 copy.44
  73.4 40.7 %all_to_all.39 = bf16[4,4,256,256]{3,2,1,0:T(8,128)(2,1)} all-to-all(bf16[4,4,256,256]{3,2,1,0:T(8,128)(2,1)S(1)} %copy.44), channel_id=1, replica_groups=mesh['y'=4,'x'=4,'z'=4,'c'=2] {'x'}, dimensions={0} | all-to-all | bytes 4194304 | tf_op jit(solution)/shard_map/all_to_all | solution.py:20
  115.6 5.1 %fusion.16 = bf16[4,768,256]{2,1,0:T(8,128)(2,1)} fusion(bf16[4,4,256,256]{3,2,1,0:T(8,128)(2,1)} %all_to_all.39, bf16[4,768,256]{2,1,0:T(8,128)(2,1)} %all-gather.8.cloned.1.call-done), kind=kOutput, calls=%fused_computation.23 | convolution fusion | flops 1611399168 | bytes 5242880 | tf_op jit(solution)/shard_map/irh,ijhd->jrd/dot_general | solution.py:43
  120.7 4.3 %all-to-all-start.3 = ((bf16[4,768,256]{2,1,0:T(8,128)(2,1)}), bf16[4,768,256]{2,1,0:T(8,128)(2,1)}, u32[]{:S(2)}, u32[]{:S(2)}) async-start(bf16[4,768,256]{2,1,0:T(8,128)(2,1)} %fusion.16), calls=%async_computation.3 | async-start | bytes 3145728 | tf_op jit(solution)/shard_map/all_to_all | solution.py:20
  125.8 19.2 %all-to-all-done.3 = bf16[4,768,256]{2,1,0:T(8,128)(2,1)} async-done(((bf16[4,768,256]{2,1,0:T(8,128)(2,1)}), bf16[4,768,256]{2,1,0:T(8,128)(2,1)}, u32[]{:S(2)}, u32[]{:S(2)}) %all-to-all-start.3) | async-done | bytes 1572896 | tf_op jit(solution)/shard_map/all_to_all | solution.py:20
  147.1 28.5 %psum.7 = f32[2,256]{1,0:T(2,128)S(1)} all-reduce(f32[2,256]{1,0:T(2,128)S(1)} %pad_maximum_fusion.1), channel_id=1, replica_groups=mesh['y'=4,'x'=4,'z'=4,'c'=2] {'y','x'}, use_global_device_ids=true, to_apply=%region_4.5 | all-reduce | flops 512 | bytes 4096 | tf_op jit(solution)/shard_map/psum | solution.py:46
  177.2 31.8 %all-gather.10.cloned.1.call-done = bf16[4,768,256]{2,1,0:T(8,128)(2,1)} async-done(((bf16[1,768,256]{2,1,0:T(8,128)(2,1)}), bf16[4,768,256]{2,1,0:T(8,128)(2,1)}) %all-gather.10.cloned.1.call-update) | async-done | bytes 1572880 | tf_op jit(solution)/shard_map/all_gather | solution.py:50
  209.0 3.9 fusion.13
  212.9 23.5 %all_to_all.40 = bf16[4,768,256]{2,1,0:T(8,128)(2,1)S(1)} all-to-all(bf16[4,768,256]{2,1,0:T(8,128)(2,1)S(1)} %fusion.13), channel_id=1, replica_groups=mesh['y'=4,'x'=4,'z'=4,'c'=2] {'x'}, dimensions={0} | all-to-all | bytes 3145728 | tf_op jit(solution)/shard_map/all_to_all | solution.py:20
  238.4 5.2 %fusion.2 = f32[4,256,4,256]{3,1,2,0:T(8,128)} fusion(bf16[4,768,256]{2,1,0:T(8,128)(2,1)} %all-gather.10.cloned.1.call-done, bf16[4,768,256]{2,1,0:T(8,128)(2,1)S(1)} %copy-done.4), kind=kOutput, calls=%fused_computation.13 | convolution fusion | flops 1610612736 | bytes 7340032 | tf_op jit(solution)/shard_map/irh,jrd->jihd/dot_general | solution.py:55
  243.6 5.4 %copy.49 = f32[4,1,2,2,256,256]{5,4,2,1,0,3:T(8,128)} copy(f32[4,1,2,2,256,256]{4,5,3,2,0,1:T(8,128)} %bitcast.168) | data formatting | bytes 8388608 | tf_op jit(solution)/shard_map/stack | solution.py:57
  249.0 14.2 %all-gather.12.cloned.1.call-done = bf16[4,768,256]{2,1,0:T(8,128)(2,1)} async-done(((bf16[1,768,256]{2,1,0:T(8,128)(2,1)}), bf16[4,768,256]{2,1,0:T(8,128)(2,1)}) %all-gather.12.cloned.1.call-update) | async-done | bytes 1572880 | tf_op jit(solution)/shard_map/all_gather | solution.py:54
  263.2 5.2 %fusion.4 = f32[4,256,4,256]{3,1,2,0:T(8,128)} fusion(bf16[4,768,256]{2,1,0:T(8,128)(2,1)} %all-gather.12.cloned.1.call-done, bf16[4,768,256]{2,1,0:T(8,128)(2,1)S(1)} %copy-done.3), kind=kOutput, calls=%fused_computation.15 | convolution fusion | flops 1610612736 | bytes 7340032 | tf_op jit(solution)/shard_map/jrd,irh->jidh/dot_general | solution.py:56
  268.4 5.3 %copy.48 = f32[4,1,2,2,256,256]{5,4,2,1,0,3:T(8,128)} copy(f32[4,1,2,2,256,256]{4,5,0,3,2,1:T(8,128)} %bitcast.169) | data formatting | bytes 8388608 | tf_op jit(solution)/shard_map/stack | solution.py:57
  273.6 7.6 %maximum_bitcast_fusion = f32[2,4,2,2,256,256]{5,4,3,2,1,0:T(8,128)} fusion(f32[4,1,2,2,256,256]{5,4,2,1,0,3:T(8,128)} %copy.49, f32[4,1,2,2,256,256]{5,4,2,1,0,3:T(8,128)} %copy.48), kind=kLoop, calls=%fused_computation | loop fusion | flops 2097152 | bytes 16777216 | tf_op jit(solution)/shard_map/transpose | solution.py:58
  281.2 8.4 %reshape.194 = f32[2,4,262144]{2,1,0:T(4,128)} reshape(f32[2,4,2,2,256,256]{5,4,3,2,1,0:T(8,128)} %maximum_bitcast_fusion) | data formatting | bytes 16777216 | tf_op jit(solution)/shard_map/reshape | solution.py:59
  289.6 26.2 %all-reduce.2 = bf16[2,4,262144]{2,1,0:T(4,128)(2,1)} all-reduce(f32[2,4,262144]{2,1,0:T(4,128)} %reshape.194), channel_id=2, replica_groups=mesh['y'=4,'x'=4,'z'=4,'c'=2] {'c'}, use_global_device_ids=true, to_apply=%region_6.7.clone | all-reduce | flops 2097152 | bytes 12582912
  315.7 2.6 fusion
  318.9 4.6 %reduce.3 = bf16[4,262144]{1,0:T(4,128)(2,1)} reduce(bf16[4,1,262144]{2,0,1:T(4,128)(2,1)S(1)} %fusion, bf16[]{:T(256)} %broadcast.101), dimensions={1}, to_apply=%copy.50.reduce_sub_computation | reduce | bytes 4194306 | tf_op jit(solution)/shard_map/convert_element_type | solution.py:24
  323.5 5.0 %reshape.207 = bf16[4,2,131072]{2,1,0:T(2,128)(2,1)} reshape(bf16[4,262144]{1,0:T(4,128)(2,1)} %reduce.3) | data formatting | bytes 4194304
  328.5 30.3 %all_to_all.41 = bf16[4,2,131072]{2,1,0:T(2,128)(2,1)S(1)} all-to-all(bf16[4,2,131072]{2,1,0:T(2,128)(2,1)} %reshape.207), channel_id=1, replica_groups=mesh['y'=4,'x'=4,'z'=4,'c'=2] {'z'}, dimensions={0} | all-to-all | bytes 4194304 | tf_op jit(solution)/shard_map/all_to_all | solution.py:20
  358.9 3.4 reshape.208
  362.2 11.9 %convert_reduce_fusion = bf16[262144]{0:T(1024)(128)(2,1)S(1)} fusion(bf16[4,1,262144]{2,1,0:T(2,128)(2,1)} %reshape.208), kind=kLoop, calls=%fused_computation.2 | loop fusion | flops 1835008 | bytes 2621440 | tf_op jit(solution)/shard_map/reduce_sum | solution.py:25
  375.1 10.9 %all-gather.14.cloned.1.call-done = bf16[2,2,2,256,256]{4,3,2,1,0:T(8,128)(2,1)} async-done(((bf16[1,2,2,256,256]{4,3,2,1,0:T(8,128)(2,1)}), bf16[2,2,2,256,256]{4,3,2,1,0:T(8,128)(2,1)}) %all-gather.14.cloned.1.call-update) | async-done | bytes 1048592 | tf_op jit(solution)/shard_map/all_gather | solution.py:61
  387.8 7.4 %reduce.4 = bf16[4,131072]{1,0:T(4,128)(2,1)S(1)} reduce(bf16[4,1,131072]{2,1,0:T(2,128)(2,1)S(1)} %convert_element_type.130, bf16[]{:T(256)} %broadcast.101), dimensions={1}, to_apply=%convert_element_type.130.reduce_sub_computation | reduce | bytes 2097154 | tf_op jit(solution)/shard_map/convert_element_type | solution.py:63
  397.3 4.3 all-to-all-start.6
  401.7 14.7 %all-to-all-done.6 = bf16[4,2,65536]{2,1,0:T(2,128)(2,1)S(1)} async-done(((bf16[4,2,65536]{2,1,0:T(2,128)(2,1)}), bf16[4,2,65536]{2,1,0:T(2,128)(2,1)S(1)}, u32[]{:S(2)}, u32[]{:S(2)}) %all-to-all-start.6) | async-done | bytes 1048608 | tf_op jit(solution)/shard_map/all_to_all | solution.py:20
  417.3 6.4 %convert_reduce_fusion.4 = f32[4,131072]{1,0:T(4,128)S(1)} fusion(bf16[4,1,131072]{2,1,0:T(2,128)(2,1)S(1)} %reshape.210), kind=kLoop, calls=%fused_computation.11 | loop fusion | flops 524288 | bytes 3145728 | tf_op jit(solution)/shard_map/convert_element_type | solution.py:63
  (51 shorter events, 20.4 us)
Async XLA Ops:
  7.2 2.5 copy-start.1
  7.2 32.7 %all-gather.6.cloned.1.call-start = ((), (), s32[]{:S(2)}) async-start(), calls=%async_computation.7 | async-start | bytes 1966080 | tf_op jit(solution)/shard_map/all_gather | solution.py:39
  9.6 106.0 %all-gather.8.cloned.1.call-start = ((), (), s32[]{:S(2)}) async-start(), calls=%async_computation.8 | async-start | bytes 1966080 | tf_op jit(solution)/shard_map/all_gather | solution.py:42
  66.4 1.7 copy-start.2
  120.7 24.3 %all-to-all-start.3 = ((bf16[4,768,256]{2,1,0:T(8,128)(2,1)}), bf16[4,768,256]{2,1,0:T(8,128)(2,1)}, u32[]{:S(2)}, u32[]{:S(2)}) async-start(bf16[4,768,256]{2,1,0:T(8,128)(2,1)} %fusion.16), calls=%async_computation.3 | async-start | bytes 3145728 | tf_op jit(solution)/shard_map/all_to_all | solution.py:20
  125.1 83.9 %all-gather.10.cloned.1.call-start = ((), (), s32[]{:S(2)}) async-start(), calls=%async_computation.9 | async-start | bytes 1966080 | tf_op jit(solution)/shard_map/all_gather | solution.py:50
  125.8 21.1 %copy-start = (f32[3,256,256]{2,1,0:T(8,128)S(1)}, f32[3,256,256]{2,1,0:T(8,128)}, u32[]{:S(2)}) copy-start(f32[3,256,256]{2,1,0:T(8,128)} %param.6) | copy-start | bytes 2359300
  177.1 86.1 %all-gather.12.cloned.1.call-start = ((), (), s32[]{:S(2)}) async-start(), calls=%async_computation.10 | async-start | bytes 1966080 | tf_op jit(solution)/shard_map/all_gather | solution.py:54
  236.3 1.5 copy-start.5
  236.3 2.1 copy-start.4
  237.6 148.5 %all-gather.14.cloned.1.call-start = ((), (), s32[]{:S(2)}) async-start(), calls=%async_computation.11 | async-start | bytes 1572864 | tf_op jit(solution)/shard_map/all_gather | solution.py:61
  243.6 19.6 %copy-start.3 = (bf16[4,768,256]{2,1,0:T(8,128)(2,1)S(1)}, bf16[4,768,256]{2,1,0:T(8,128)(2,1)}, u32[]{:S(2)}) copy-start(bf16[4,768,256]{2,1,0:T(8,128)(2,1)} %all-gather.6.cloned.1.call-done) | copy-start | bytes 4718596
  397.3 19.0 %all-to-all-start.6 = ((bf16[4,2,65536]{2,1,0:T(2,128)(2,1)}), bf16[4,2,65536]{2,1,0:T(2,128)(2,1)S(1)}, u32[]{:S(2)}, u32[]{:S(2)}) async-start(bf16[4,2,65536]{2,1,0:T(2,128)(2,1)} %reshape.209), calls=%async_computation.6 | async-start | bytes 2097152 | tf_op jit(solution)/shard_map/all_to_all | solution.py:20
Sparse Core Ops, SparseCore 0:
  10.2 29.4 all-gather.5
  67.8 47.8 all-gather.7
  177.2 31.6 all-gather.9
  237.7 25.4 all-gather.11
  375.3 10.7 all-gather.13

commit v2 on v1

v2 whole, which is shorter than its diff:
```python
import math

import jax
import jax.numpy as jnp
from jax import lax
from jax.experimental import pallas as pl
from jax.experimental.pallas import tpu as pltpu
from jax.sharding import Mesh
from jax.sharding import PartitionSpec as P

D = 4096
STEPS = 3
B = 256
H = B // 2
DIM = ("y", "x")
BATCH = ("z", "c")
MESH = pl.DeviceIdType.MESH
f32, bf16 = jnp.float32, jnp.bfloat16

time_step = 1.0 / 64.0
lam_coef = 50.0
noise_coef = math.sqrt(2.0)
zscale = 2.0 / math.sqrt(D)
COPIES = 240


def place(pos, extent):
    return pl.ds(pl.multiple_of(pos * extent, extent), extent)


class Net:
    def __init__(self, send, recv):
        self.send, self.recv, self.count, self.begun = send, recv, 0, []

    def copy(self, src, dst, device):
        k = self.count
        self.count += 1
        assert self.count <= COPIES
        return pltpu.make_async_remote_copy(
            src_ref=src,
            dst_ref=dst,
            send_sem=self.send.at[k],
            recv_sem=self.recv.at[k],
            device_id=device,
            device_id_type=MESH,
        )

    def start(self, copy):
        copy.start()
        self.begun.append(copy)

    def drain(self):
        for copy in self.begun:
            copy.wait_send()


class Gather:
    def __init__(self, net, axis, view):
        p = lax.axis_index(axis)
        r, l = lax.rem(p + 1, 4), lax.rem(p + 3, 4)
        self.net = net
        self.copies = [
            net.copy(view(owner, half), view(owner, half), {axis: to})
            for owner, half, to in ((p, 0, r), (p, 1, l), (p, 1, r), (p, 0, l), (l, 0, r), (r, 1, l))
        ]

    def start(self):
        for k in range(4):
            self.net.start(self.copies[k])

    def mid(self):
        for k in range(2):
            self.copies[k].wait_recv()
            self.net.start(self.copies[4 + k])

    def finish(self):
        for k in range(2, 6):
            self.copies[k].wait_recv()


class Scatter:
    def __init__(self, net, axis, sent, far, near, held):
        p = lax.axis_index(axis)
        r, l = {axis: lax.rem(p + 1, 4)}, {axis: lax.rem(p + 3, 4)}
        self.net, self.sent, self.far, self.near, self.held = net, sent, far, near, held
        self.copies = {
            (2, 0): net.copy(sent.at[1, 0], far.at[0], r),
            (2, 1): net.copy(sent.at[1, 1], far.at[1], l),
            (1, 1): net.copy(sent.at[0, 1], near.at[0, 1], r),
            (3, 0): net.copy(sent.at[2, 0], near.at[1, 0], l),
            (1, 0): net.copy(sent.at[0, 0], near.at[0, 0], r),
            (3, 1): net.copy(sent.at[2, 1], near.at[1, 1], l),
        }

    def put(self, k, half, value):
        if (k, half) in ((2, 0), (2, 1), (1, 1), (3, 0)):
            self.sent[k - 1, half] = value.astype(bf16)
            self.net.start(self.copies[k, half])
        else:
            self.held[{0: half, 1: 2, 3: 3}[k]] = value

    def mid(self):
        for side, key in enumerate(((1, 0), (3, 1))):
            self.copies[2, side].wait_recv()
            k, half = key
            self.sent[k - 1, half] = (self.held[2 + side] + self.far[side].astype(f32)).astype(bf16)
            self.net.start(self.copies[key])

    def finish(self):
        for key in ((1, 1), (3, 0), (1, 0), (3, 1)):
            self.copies[key].wait_recv()
        near = self.near
        return [self.held[half] + near[0, half].astype(f32) + near[1, half].astype(f32) for half in range(2)]


ORDER = (2, 1, 3, 0)


def dot(a, b, dims):
    return lax.dot_general(a, b, (dims, ((), ())), preferred_element_type=f32)


def kernel(
    start, inc, w_in, w_out, initial,
    res_out, gin_out, gout_out,
    xs, acts, us, scaled, ghs, w1, w2, slopes,
    sent, far, near, held, acc, other, zsent, zfar, zheld, znear,
    leave, arrive, totals, rowres, send, recv, local,
):
    y, x, z, c = (lax.axis_index(a) for a in ("y", "x", "z", "c"))

    barrier = pltpu.get_barrier_semaphore()
    peers = [{a: lax.rem(i + k, 4)} for a, i in (("x", x), ("y", y)) for k in (1, 2, 3)]
    peers += [{"z": lax.rem(z + k, 4)} for k in (1, 3)]
    peers += [{"c": 1 - c}] + [{"x": lax.rem(x + k, 4), "c": 1 - c} for k in (1, 2, 3)]
    for peer in peers:
        pl.semaphore_signal(barrier, inc=1, device_id=peer, device_id_type=MESH)

    locals_ = [pltpu.make_async_copy(w_in.at[:, x], w1.at[x], local.at[0])]
    for j in range(4):
        locals_.append(
            pltpu.make_async_copy(w_out.at[:, :, pl.ds(pl.multiple_of(1024 * j + x * B, B), B)], w2.at[j, x], local.at[1 + j])
        )
    for copy in locals_:
        copy.start()

    state = start[...]
    for n in range(STEPS):
        xs[pl.ds(n * B, B), place(y, B)] = state.astype(bf16)
        state = state + noise_coef * inc[n]
    norm = state * state

    net = Net(send, recv)

    def blocks(ref, n):
        return lambda owner, half: ref.at[pl.ds(n * B + half * H, H), place(owner, B)]

    def quarter(ref, first):
        if first:
            return lambda i: lambda owner, half: ref.at[i, owner, c, pl.ds(half * 64, 64)]
        return lambda i: lambda owner, half: ref.at[owner, i, c, pl.ds(half * 64, 64)]

    gx = [Gather(net, "y", blocks(xs, n)) for n in range(STEPS)]
    others = [lax.rem(x + k, 4) for k in (1, 2, 3)]
    w1s = [net.copy(w_in.at[z, i, c], w1.at[x, z, c], {"x": i}) for i in others]
    w2s = [
        net.copy(w_out.at[c, :, pl.ds(pl.multiple_of(z * 1024 + i * B, B), B)], w2.at[z, x, c], {"x": i}) for i in others
    ]
    froms = [lax.rem(x + 4 - k, 4) for k in (1, 2, 3)]
    wz1 = [Gather(net, "z", quarter(w1, True)(i)) for i in froms]
    wz2 = [Gather(net, "z", quarter(w2, False)(i)) for i in froms]
    d1 = [net.copy(w1.at[i, :, c], w1.at[i, :, c], {"c": 1 - c}) for i in froms]
    d2 = [net.copy(w2.at[:, i, c], w2.at[:, i, c], {"c": 1 - c}) for i in froms]

    def scatter(axis, k):
        return Scatter(net, axis, sent.at[k], far.at[k], near.at[k], held.at[k])

    sh = [scatter("x", n) for n in range(STEPS)]
    sz = [scatter("y", 3 + n) for n in range(STEPS)]
    sg = [scatter("x", 6 + n) for n in range(STEPS)]
    ga = [Gather(net, "x", blocks(acts, n)) for n in range(STEPS)]
    gu = [Gather(net, "y", blocks(us, n)) for n in range(STEPS)]
    gg = [Gather(net, "x", blocks(ghs, n)) for n in range(STEPS)]
    ty = [net.copy(totals.at[0, y], totals.at[0, y], {"y": lax.rem(y + k, 4)}) for k in (1, 2, 3)]
    tx = [net.copy(totals.at[1, x], totals.at[1, x], {"x": lax.rem(x + k, 4)}) for k in (1, 2, 3)]

    pl.semaphore_wait(barrier, len(peers))
    for copy in w1s:
        net.start(copy)
    gx[0].start()
    for copy in w2s:
        net.start(copy)
    gx[1].start()
    gx[2].start()

    def rows(ref, n):
        return ref[pl.ds(n * B, B), :]

    def first(n):
        for k in ORDER:
            w = w1[lax.rem(x + k, 4)].reshape(4 * B, B)
            part = dot(rows(xs, n), w, ((1,), (0,)))
            for half in range(2):
                sh[n].put(k, half, part[half * H : half * H + H])

    def second(n):
        for k in ORDER:
            w = w2[lax.rem(y + k, 4)].reshape(4 * B, B)
            part = dot(rows(acts, n), w, ((1,), (0,)))
            for half in range(2):
                sz[n].put(k, half, part[half * H : half * H + H])

    def third(n):
        for k in ORDER:
            i = lax.rem(x + k, 4)
            part = None
            for j in range(4):
                term = dot(us[pl.ds(n * B, B), pl.ds(j * B, B)], w2[j, i].reshape(B, B), ((1,), (1,)))
                part = term if part is None else part + term
            for half in range(2):
                sg[n].put(k, half, part[half * H : half * H + H])

    def activate(n):
        for half, h in enumerate(sh[n].finish()):
            sig = jax.nn.sigmoid(h)
            acts[pl.ds(n * B + half * H, H), place(x, B)] = (h * sig).astype(bf16)
            slopes[n, half] = sig * (1.0 + h * (1.0 - sig))
        ga[n].start()

    terms = [0.0, 0.0]

    def control(n):
        for half, total in enumerate(sz[n].finish()):
            zval = zscale * total
            dw = inc[n, pl.ds(half * H, H), :]
            us[pl.ds(n * B + half * H, H), place(y, B)] = (zscale * (lam_coef * time_step * zval + dw)).astype(bf16)
            term = 0.5 * lam_coef * time_step * zval * zval + zval * dw
            terms[half] = terms[half] + (term[:, :128] + term[:, 128:])
        gu[n].start()

    def hidden_grad(n):
        for half, g in enumerate(sg[n].finish()):
            r = rowres[pl.ds(half * H, H), :]
            r = jnp.concatenate([r, r], axis=1)
            ghs[pl.ds(n * B + half * H, H), place(x, B)] = (r * g * slopes[n, half]).astype(bf16)
        gg[n].start()

    for k in range(3):
        w1s[k].wait_recv()
        wz1[k].start()
    gx[0].mid()
    for k in range(3):
        wz1[k].mid()
    for k in range(3):
        w2s[k].wait_recv()
        wz2[k].start()
    gx[1].mid()
    gx[2].mid()
    for k in range(3):
        wz1[k].finish()
        net.start(d1[k])
    gx[0].finish()
    locals_[0].wait()
    for k in range(3):
        d1[k].wait_recv()
    first(0)
    for k in range(3):
        wz2[k].mid()
    gx[1].finish()
    first(1)
    sh[0].mid()
    gx[2].finish()
    first(2)
    sh[1].mid()
    activate(0)
    sh[2].mid()
    for k in range(3):
        wz2[k].finish()
        net.start(d2[k])
    activate(1)
    ga[0].mid()
    activate(2)
    ga[1].mid()
    for copy in locals_[1:]:
        copy.wait()
    for k in range(3):
        d2[k].wait_recv()
    ga[0].finish()
    second(0)
    ga[2].mid()
    ga[1].finish()
    second(1)
    sz[0].mid()
    ga[2].finish()
    second(2)
    sz[1].mid()
    control(0)
    sz[2].mid()
    control(1)
    gu[0].mid()
    control(2)

    def per_path(t):
        return jnp.sum(t.T, axis=0, keepdims=True)

    y_row = per_path(jnp.concatenate(terms, axis=0))
    n_row = per_path(norm[:, :128] + norm[:, 128:])
    totals[0, y] = jnp.concatenate([y_row, n_row, jnp.zeros((6, B), f32)], axis=0)
    for copy in ty:
        net.start(copy)
    gu[1].mid()
    gu[0].finish()
    third(0)
    for copy in ty:
        copy.wait_recv()
    totals[1, x] = totals[0, 0] + totals[0, 1] + totals[0, 2] + totals[0, 3]
    for copy in tx:
        net.start(copy)
    gu[2].mid()
    gu[1].finish()
    third(1)
    sg[0].mid()
    for copy in tx:
        copy.wait_recv()
    both = totals[1, 0] + totals[1, 1] + totals[1, 2] + totals[1, 3]
    residual = initial[0] + both[0:1] - jnp.log((1.0 + both[1:2]) * 0.5)
    res_out[...] = residual
    rowres[...] = jnp.broadcast_to(residual, (128, B)).T
    gu[2].finish()
    third(2)
    sg[1].mid()
    hidden_grad(0)
    sg[2].mid()
    hidden_grad(1)
    gg[0].mid()

    swap = {}
    zs = []
    for g in range(2):
        for k in ORDER:
            cols = place(lax.rem(z + k, 4), B)
            for e in range(2):
                swap[g, k, e] = net.copy(acc.at[g, 2 * (1 - c) + e, :, cols], other.at[g, e, :, cols], {"c": 1 - c})
        zs.append(Scatter(net, "z", zsent.at[g], zfar.at[g], znear.at[g], zheld.at[g]))

    def exchange(g):
        for k in ORDER:
            for e in range(2):
                net.start(swap[g, k, e])

    def over_z(g):
        for k in ORDER:
            cols = place(lax.rem(z + k, 4), B)
            for e in range(2):
                swap[g, k, e].wait_recv()
                zs[g].put(k, e, acc[g, 2 * c + e, :, cols] + other[g, e, :, cols])

    def to_owner(g):
        outs = []
        for e, value in enumerate(zs[g].finish()):
            value = value.T if g == 0 else value
            i = 2 * c + e
            leave[g, e] = value
            outs.append(
                pltpu.make_async_remote_copy(
                    src_ref=leave.at[g, e],
                    dst_ref=arrive.at[g, lax.rem(x, 2)],
                    send_sem=send.at[COPIES + 2 * g + e],
                    recv_sem=recv.at[COPIES + 2 * g + lax.rem(x, 2)],
                    device_id={"x": i, "c": x // 2},
                    device_id_type=MESH,
                )
            )

            @pl.when(i != x)
            def _(copy=outs[e]):
                copy.start()

            @pl.when(i == x)
            def _(e=e):
                arrive[g, e] = leave[g, e]

        return outs

    def collect(g, outs):
        target = (gin_out, gout_out)[g]
        puts = []
        for t in range(2):

            @pl.when(2 * c + t != x)
            def _(t=t):
                pltpu.make_async_remote_copy(
                    src_ref=leave.at[g, t],
                    dst_ref=arrive.at[g, t],
                    send_sem=send.at[COPIES + 2 * g + t],
                    recv_sem=recv.at[COPIES + 2 * g + t],
                    device_id={"x": 2 * c + t, "c": x // 2},
                    device_id_type=MESH,
                ).wait_recv()

            dst = target.at[pl.ds(t * B, B), :] if g == 0 else target.at[:, pl.ds(t * B, B)]
            copy = pltpu.make_async_copy(arrive.at[g, t], dst, local.at[8 + 2 * g + t])
            copy.start()
            puts.append(copy)
        for e in range(2):

            @pl.when(2 * c + e != x)
            def _(copy=outs[e]):
                copy.wait_send()

        return puts

    halves = [2 * (1 - c), 2 * (1 - c) + 1, 2 * c, 2 * c + 1]
    for n in range(STEPS):
        for k in range(8):
            lanes = pl.ds(k * 128, 128)
            scaled[pl.ds(n * B, B), lanes] = (us[pl.ds(n * B, B), lanes].astype(f32) * rowres[...]).astype(bf16)
    for i in halves:
        acc[1, i] = dot(acts[:, place(i, B)], scaled[...], ((0,), (0,)))
    exchange(1)
    hidden_grad(2)
    gg[1].mid()
    over_z(1)
    gg[0].finish()
    gg[1].finish()
    gg[2].mid()
    two = pl.ds(0, 2 * B)
    for i in halves:
        acc[0, i] = dot(ghs[two, place(i, B)], xs[two, :], ((0,), (0,)))
    zs[1].mid()
    gg[2].finish()
    last = pl.ds(2 * B, B)
    for i in halves:
        acc[0, i] += dot(ghs[last, place(i, B)], xs[last, :], ((0,), (0,)))
    exchange(0)
    over_z(0)
    outs1 = to_owner(1)
    zs[0].mid()
    puts = collect(1, outs1)
    outs0 = to_owner(0)
    puts += collect(0, outs0)
    for copy in puts:
        copy.wait()
    net.drain()


def on_device(start, increments, w_in, w_out, initial):
    vmem, anywhere = pl.BlockSpec(memory_space=pltpu.VMEM), pl.BlockSpec(memory_space=pl.ANY)
    stacked = pltpu.VMEM((STEPS * B, 4 * B), bf16)
    weights = pltpu.VMEM((4, 4, 2, H, B), bf16)
    residual, grad_in, grad_out = pl.pallas_call(
        kernel,
        out_shape=(
            jax.ShapeDtypeStruct((1, B), f32),
            jax.ShapeDtypeStruct((2 * B, B), f32),
            jax.ShapeDtypeStruct((B, 2 * B), f32),
        ),
        in_specs=[vmem, vmem, anywhere, anywhere, pl.BlockSpec(memory_space=pltpu.SMEM)],
        out_specs=(vmem, anywhere, anywhere),
        scratch_shapes=[
            stacked,
            stacked,
            stacked,
            stacked,
            stacked,
            weights,
            weights,
            pltpu.VMEM((STEPS, 2, H, B), f32),
            pltpu.VMEM((9, 3, 2, H, B), bf16),
            pltpu.VMEM((9, 2, H, B), bf16),
            pltpu.VMEM((9, 2, 2, H, B), bf16),
            pltpu.VMEM((9, 4, H, B), f32),
            pltpu.VMEM((2, 4, B, 4 * B), f32),
            pltpu.VMEM((2, 2, B, 4 * B), f32),
            pltpu.VMEM((2, 3, 2, B, B), bf16),
            pltpu.VMEM((2, 2, B, B), bf16),
            pltpu.VMEM((2, 4, B, B), f32),
            pltpu.VMEM((2, 2, 2, B, B), bf16),
            pltpu.VMEM((2, 2, B, B), f32),
            pltpu.VMEM((2, 2, B, B), f32),
            pltpu.VMEM((2, 4, 8, B), f32),
            pltpu.VMEM((B, 128), f32),
            pltpu.SemaphoreType.DMA((COPIES + 4,)),
            pltpu.SemaphoreType.DMA((COPIES + 4,)),
            pltpu.SemaphoreType.DMA((12,)),
        ],
        compiler_params=pltpu.CompilerParams(collective_id=0, has_side_effects=True, vmem_limit_bytes=66000000),
    )(start, increments, w_in.reshape(4, 4, 2, H, B), w_out.reshape(2, H, D), initial.reshape(1))
    return residual.reshape(B), grad_in, grad_out


def solution(mesh):
    finer = Mesh(mesh.devices.reshape(4, 4, 4, 2), ("y", "x", "z", "c"))
    return jax.shard_map(
        on_device,
        mesh=finer,
        in_specs=(P(BATCH, DIM), P(None, BATCH, DIM), P(None, DIM), P(DIM, None), P()),
        out_specs=(P(BATCH), P(BATCH, DIM), P(DIM, BATCH)),
        check_vma=False,
    )
```

time: 440 us -> 138 us (0.31); the launches traced: 433 us -> 138 us
  blocking collectives: 203 us -> 0 us
  Pallas kernels: 0 us -> 131 us
  waiting for transfers between devices: 92.5 us -> 0 us
  other arithmetic: 46.3 us -> 0 us
  local copies, waits for them, and re-layouts: 45.3 us -> 4.98 us
  matrix products: 22.5 us -> 0 us
  between operations: 15.1 us -> 1.29 us
  starting transfers between devices: 9.04 us -> 0 us
    all_to_all x5 -> x0, blocking collectives: 148 us -> none  [a2a(): return lax.all_to_all(array, axis, split_axis=0, concat_axis=0, tiled=True)]
    pallas_call x0 -> x1, Pallas kernels: none -> 131 us  [on_device(): pl.pallas_call(kernel, out_shape=(jax.ShapeDtypeStruct((1, B), f32), jax....]
    all_gather x5 -> x0, waiting for transfers between devices: 58.5 us -> none  [the longest x1 31.8 us: on_device(): gg = lax.all_gather(gz, 'y')]
    all_to_all x2 -> x0, waiting for transfers between devices: 33.9 us -> none  [a2a(): return lax.all_to_all(array, axis, split_axis=0, concat_axis=0, tiled=True)]
    psum x1 -> x0, blocking collectives: 28.5 us -> none  [on_device(): both = lax.psum(jnp.stack([terms, norm]), DIM)]
    unnamed x1 -> x0, blocking collectives: 26.2 us -> none
    dot_general x5 -> x0, matrix products: 22.5 us -> none  [the longest x1 5.16 us: on_device(): gin = jnp.einsum('jrd,irh->jidh', xg, hg, preferred_element_type=f32)]
    convert_element_type x6 -> x0, other arithmetic: 21.4 us -> none  [the longest x1 7.44 us: on_device(): grads.astype(bf16)]
  transfers between devices with their start and end apart: 7 -> 0, of which waited for: 6 -> 0; matrix products, arithmetic and copies ran while one was open for 4% -> 0% of each run, Pallas kernels for 0% -> 0%
where the time goes in v2:
time: 138 us
  Pallas kernels  131 us (95%)
  local copies, waits for them, and re-layouts  4.98 us (4%)
    pallas_call x1, Pallas kernels, on_device(): pl.pallas_call(kernel, out_shape=(jax.ShapeDtypeStruct((1, B), f32), jax....  131 us
    unnamed x3, local copies, waits for them, and re-layouts  4.98 us

profile of v2, /device:TPU:1, one launch (start us, length us, event | category | flops | bytes accessed | tf_op | source)
XLA Modules:
  0.0 137.7 jit_solution(1912827560668627637)
XLA Ops:
  1.3 131.4 %shard_map.76 = (f32[1,256]{1,0:T(1,128)}, f32[512,256]{1,0:T(8,128)}, f32[256,512]{1,0:T(8,128)}) custom-call(f32[256,256]{1,0:T(8,128)} %start.1, f32[3,256,256]{2,1,0:T(8,128)} %inc.1, bf16[4,4,2,128,256]{4,3,2,1,0:T(8,128)(2,1)} %bitcast.5, bf16[2,128,4096]{2,1,0:T(8,128)(2,1)} %bitcast.6, f32[1]{0:T(128)} %bitcast.4.initial), custom_call_target="tpu_custom_call" | custom-call | tf_op jit(solution)/shard_map/pallas_call | solution.py:451
  132.7 1.2 copy.12
  133.9 1.9 %copy.13 = f32[512,256]{1,0:T(8,128)} copy(f32[512,256]{1,0:T(8,128)} %get-tuple-element.13) | data formatting | bytes 1048576
  135.8 1.9 %copy.14 = f32[256,512]{1,0:T(8,128)} copy(f32[256,512]{1,0:T(8,128)} %get-tuple-element.14) | data formatting | bytes 1048576

commit v3 on v1

v3 whole, which is shorter than its diff:
```python
import math

import jax
import jax.numpy as jnp
from jax import lax
from jax.experimental import pallas as pl
from jax.experimental.pallas import tpu as pltpu
from jax.sharding import Mesh
from jax.sharding import PartitionSpec as P

D = 4096
STEPS = 3
B = 256
H = B // 2
DIM = ("y", "x")
BATCH = ("z", "c")
MESH = pl.DeviceIdType.MESH
f32, bf16 = jnp.float32, jnp.bfloat16

time_step = 1.0 / 64.0
lam_coef = 50.0
noise_coef = math.sqrt(2.0)
zscale = 2.0 / math.sqrt(D)
COPIES = 250


def place(pos, extent):
    return pl.ds(pl.multiple_of(pos * extent, extent), extent)


class Net:
    def __init__(self, send, recv):
        self.send, self.recv, self.count, self.begun, self.seen = send, recv, 0, [], set()

    def copy(self, src, dst, device):
        k = self.count
        self.count += 1
        assert self.count <= COPIES
        return pltpu.make_async_remote_copy(
            src_ref=src,
            dst_ref=dst,
            send_sem=self.send.at[k],
            recv_sem=self.recv.at[k],
            device_id=device,
            device_id_type=MESH,
        )

    def start(self, copy):
        copy.start()
        self.begun.append(copy)

    def arrived(self, copy):
        if id(copy) not in self.seen:
            self.seen.add(id(copy))
            copy.wait_recv()

    def drain(self):
        for copy in self.begun:
            copy.wait_send()


class Gather:
    def __init__(self, net, axis, view):
        p = lax.axis_index(axis)
        r, l = lax.rem(p + 1, 4), lax.rem(p + 3, 4)
        self.net = net
        self.copies = [
            net.copy(view(owner, half), view(owner, half), {axis: to})
            for owner, half, to in ((p, 0, r), (p, 1, l), (p, 1, r), (p, 0, l), (l, 0, r), (r, 1, l))
        ]

    def start(self):
        for k in range(4):
            self.net.start(self.copies[k])

    def mid(self):
        for k in range(2):
            self.net.arrived(self.copies[k])
            self.net.start(self.copies[4 + k])

    def finish(self):
        for k in range(2, 6):
            self.net.arrived(self.copies[k])


class Scatter:
    def __init__(self, net, axis, sent, far, near, held):
        p = lax.axis_index(axis)
        r, l = {axis: lax.rem(p + 1, 4)}, {axis: lax.rem(p + 3, 4)}
        self.net, self.sent, self.far, self.near, self.held = net, sent, far, near, held
        self.copies = {
            (2, 0): net.copy(sent.at[1, 0], far.at[0], r),
            (2, 1): net.copy(sent.at[1, 1], far.at[1], l),
            (1, 1): net.copy(sent.at[0, 1], near.at[0, 1], r),
            (3, 0): net.copy(sent.at[2, 0], near.at[1, 0], l),
            (1, 0): net.copy(sent.at[0, 0], near.at[0, 0], r),
            (3, 1): net.copy(sent.at[2, 1], near.at[1, 1], l),
        }

    def put(self, k, half, value):
        if (k, half) in ((2, 0), (2, 1), (1, 1), (3, 0)):
            self.sent[k - 1, half] = value.astype(bf16)
            self.net.start(self.copies[k, half])
        else:
            self.held[{0: half, 1: 2, 3: 3}[k]] = value

    def mid(self):
        for side, key in enumerate(((1, 0), (3, 1))):
            self.copies[2, side].wait_recv()
            k, half = key
            self.sent[k - 1, half] = (self.held[2 + side] + self.far[side].astype(f32)).astype(bf16)
            self.net.start(self.copies[key])

    def finish(self):
        for key in ((1, 1), (3, 0), (1, 0), (3, 1)):
            self.copies[key].wait_recv()
        near = self.near
        return [self.held[half] + near[0, half].astype(f32) + near[1, half].astype(f32) for half in range(2)]


ORDER = (2, 1, 3, 0)
PROGRAM = [
    "w1a2", "gx0.mid", "w1a1", "w1a0", "w1b1", "w1b2", "w1b0", "w2a1", "gx1.mid", "gx2.mid", "w1c1", "w1c2", "f02",
    "w2b1", "w2a2", "w1c0", "f01", "f12", "f03", "sh0.mid", "w2a0", "f11", "f13", "w2b0", "w2b2", "w2c1", "sh1.mid",
    "f00", "f10", "act0", "ga0.mid", "w2c2", "act1", "w2c0", "s02", "s03", "s01", "ga1.mid", "f22", "f21", "s00",
    "sz0.mid", "f20", "f23", "s12", "s13", "sh2.mid", "s11", "sz1.mid", "con0", "s10", "act2", "con1", "ga2.mid",
    "gu0.mid", "s22", "s23", "s21", "t02", "sz2.mid", "t01", "s20", "t00", "gu1.mid", "t03", "con2", "sg0.mid", "t12",
    "t13", "t11", "tot", "gu2.mid", "sg1.mid", "tot2", "t22", "t23", "t21", "res", "hid0", "sc0", "t10", "sc1", "t20",
    "sg2.mid", "sc2", "hid1", "go1", "gg0.mid", "go2", "po0", "po2", "po3", "hid2", "gg1.mid", "po1", "gg2.mid",
    "zo.mid", "gi1", "gi2", "gi3", "pi2", "pi1", "pi3", "zi.mid", "zo.fin", "pi0", "zi.fin", "colo", "coli",
]


def dot(a, b, dims):
    return lax.dot_general(a, b, (dims, ((), ())), preferred_element_type=f32)


def kernel(
    start_in, inc_in, w_in, w_out, initial,
    res_out, grads_out,
    start, inc, xs, acts, us, scaled, ghs, w1, w2, slopes,
    sent, far, near, held, acc, other, zsent, zfar, zheld, znear,
    leave, totals, nrow, folded, rowres, send, recv, local,
):
    y, x, z, c = (lax.axis_index(a) for a in ("y", "x", "z", "c"))

    barrier = pltpu.get_barrier_semaphore()
    peers = [{a: lax.rem(i + k, 4)} for a, i in (("x", x), ("y", y)) for k in (1, 2, 3)]
    peers += [{"z": lax.rem(z + k, 4)} for k in (1, 3)]
    peers += [{"c": 1 - c}] + [{"x": lax.rem(x + k, 4), "c": 1 - c} for k in (1, 2, 3)]
    for peer in peers:
        pl.semaphore_signal(barrier, inc=1, device_id=peer, device_id_type=MESH)

    fetch = [pltpu.make_async_copy(start_in, start, local.at[0])]
    fetch += [pltpu.make_async_copy(inc_in.at[n], inc.at[n], local.at[1 + n]) for n in range(STEPS)]
    own1 = [pltpu.make_async_copy(w_in.at[:, x], w1.at[x], local.at[4])]
    own2 = []
    for j in range(4):
        cols = pl.ds(pl.multiple_of(1024 * j + x * B, B), B)
        own2.append(pltpu.make_async_copy(w_out.at[:, :, cols], w2.at[j, x], local.at[5 + j]))
    for copy in fetch + own1 + own2:
        copy.start()

    net = Net(send, recv)

    def blocks(ref, n):
        return lambda owner, half: ref.at[pl.ds(n * B + half * H, H), place(owner, B)]

    def piece(m, i, j):
        return w1.at[i, j, c] if m == 1 else w2.at[j, i, c]

    def quarter(m, i):
        return lambda owner, half: piece(m, i, owner).at[pl.ds(half * 64, 64)]

    gx = [Gather(net, "y", blocks(xs, n)) for n in range(STEPS)]
    others = [lax.rem(x + k, 4) for k in (1, 2, 3)]
    froms = [lax.rem(x + 4 - k, 4) for k in (1, 2, 3)]
    ws, wz, wd = {}, {}, {}
    for m in (1, 2):
        for k, i in enumerate(others):
            cols = pl.ds(pl.multiple_of(z * 1024 + i * B, B), B)
            src = w_in.at[z, i, c] if m == 1 else w_out.at[c, :, cols]
            ws[m, k] = net.copy(src, piece(m, x, z), {"x": i})
        for k, i in enumerate(froms):
            wz[m, k] = Gather(net, "z", quarter(m, i))
            for t in range(4):
                mine = piece(m, i, lax.rem(z + t, 4))
                wd[m, k, t] = net.copy(mine, mine, {"c": 1 - c})

    def scatter(axis, k):
        return Scatter(net, axis, sent.at[k], far.at[k], near.at[k], held.at[k])

    sh = [scatter("x", n) for n in range(STEPS)]
    sz = [scatter("y", 3 + n) for n in range(STEPS)]
    sg = [scatter("x", 6 + n) for n in range(STEPS)]
    ga = [Gather(net, "x", blocks(acts, n)) for n in range(STEPS)]
    gu = [Gather(net, "y", blocks(us, n)) for n in range(STEPS)]
    gg = [Gather(net, "x", blocks(ghs, n)) for n in range(STEPS)]
    ty = [net.copy(totals.at[0, y], totals.at[0, y], {"y": lax.rem(y + k, 4)}) for k in (1, 2, 3)]
    tx = [net.copy(totals.at[1, x], totals.at[1, x], {"x": lax.rem(x + k, 4)}) for k in (1, 2, 3)]
    swap, zs = {}, []
    for g in range(2):
        for k in ORDER:
            cols = place(lax.rem(z + k, 4), B)
            for e in range(2):
                swap[g, k, e] = net.copy(acc.at[g, 2 * (1 - c) + e, :, cols], other.at[g, e, :, cols], {"c": 1 - c})
        zs.append(Scatter(net, "z", zsent.at[g], zfar.at[g], znear.at[g], zheld.at[g]))

    def per_path(t):
        return jnp.sum(t.T, axis=0, keepdims=True)

    pl.semaphore_wait(barrier, len(peers))
    for k in (1, 0, 2):
        net.start(ws[1, k])
    fetch[0].wait()
    state = start[...]
    for n in range(STEPS):
        xs[pl.ds(n * B, B), place(y, B)] = state.astype(bf16)
        gx[n].start()
        if n == 0:
            for k in (1, 0, 2):
                net.start(ws[2, k])
        fetch[1 + n].wait()
        state = state + noise_coef * inc[n]
    norm = state * state
    nrow[...] = per_path(norm[:, :128] + norm[:, 128:])

    def rows(ref, n):
        return ref[pl.ds(n * B, B), :]

    def put_both(scatter_sum, k, part):
        for half in range(2):
            scatter_sum.put(k, half, part[half * H : half * H + H])

    ready = set()

    def wait_once(copies):
        for copy in copies:
            if id(copy) not in ready:
                ready.add(id(copy))
                copy.wait()

    def weights(m, k):
        net.arrived(ws[m, k])
        for copy in wz[m, k].copies:
            net.arrived(copy)
        for t in range(4):
            net.arrived(wd[m, k, t])

    def first(n, k):
        gx[n].finish()
        if k:
            weights(1, 3 - k)
        else:
            wait_once(own1)
        w = w1[lax.rem(x + k, 4)].reshape(4 * B, B)
        put_both(sh[n], k, dot(rows(xs, n), w, ((1,), (0,))))

    def second(n, k):
        ga[n].finish()
        for e in range(3):
            weights(2, e)
        wait_once(own2)
        w = w2[lax.rem(y + k, 4)].reshape(4 * B, B)
        put_both(sz[n], k, dot(rows(acts, n), w, ((1,), (0,))))

    def third(n, k):
        gu[n].finish()
        i = lax.rem(x + k, 4)
        part = None
        for j in range(4):
            term = dot(us[pl.ds(n * B, B), pl.ds(j * B, B)], w2[j, i].reshape(B, B), ((1,), (1,)))
            part = term if part is None else part + term
        put_both(sg[n], k, part)

    def activate(n):
        for half, h in enumerate(sh[n].finish()):
            sig = jax.nn.sigmoid(h)
            acts[pl.ds(n * B + half * H, H), place(x, B)] = (h * sig).astype(bf16)
            slopes[n, half] = sig * (1.0 + h * (1.0 - sig))
        ga[n].start()

    begun = []

    def control(n):
        for half, total in enumerate(sz[n].finish()):
            zval = zscale * total
            dw = inc[n, pl.ds(half * H, H), :]
            us[pl.ds(n * B + half * H, H), place(y, B)] = (zscale * (lam_coef * time_step * zval + dw)).astype(bf16)
            term = 0.5 * lam_coef * time_step * zval * zval + zval * dw
            term = term[:, :128] + term[:, 128:]
            folded[half] = folded[half] + term if begun else term
        begun.append(n)
        gu[n].start()

    def hidden_grad(n):
        for half, g in enumerate(sg[n].finish()):
            r = rowres[pl.ds(half * H, H), :]
            r = jnp.concatenate([r, r], axis=1)
            ghs[pl.ds(n * B + half * H, H), place(x, B)] = (r * g * slopes[n, half]).astype(bf16)
        gg[n].start()

    def totals_y():
        y_row = per_path(folded[...].reshape(B, 128))
        totals[0, y] = jnp.concatenate([y_row, nrow[...], jnp.zeros((6, B), f32)], axis=0)
        for copy in ty:
            net.start(copy)

    def totals_x():
        for copy in ty:
            net.arrived(copy)
        totals[1, x] = totals[0, 0] + totals[0, 1] + totals[0, 2] + totals[0, 3]
        for copy in tx:
            net.start(copy)

    def residuals():
        for copy in tx:
            net.arrived(copy)
        both = totals[1, 0] + totals[1, 1] + totals[1, 2] + totals[1, 3]
        residual = initial[0] + both[0:1] - jnp.log((1.0 + both[1:2]) * 0.5)
        res_out[...] = residual
        rowres[...] = jnp.broadcast_to(residual, (128, B)).T

    def scale(n):
        gu[n].finish()
        for k in range(8):
            lanes = pl.ds(k * 128, 128)
            scaled[pl.ds(n * B, B), lanes] = (us[pl.ds(n * B, B), lanes].astype(f32) * rowres[...]).astype(bf16)

    def give(g):
        for k in ORDER:
            for e in range(2):
                net.start(swap[g, k, e])

    def out_sum(core):
        for e in range(2):
            i = 2 * core + e
            acc[1, i] = dot(acts[:, place(i, B)], scaled[...], ((0,), (0,)))

    def in_sum(core, first_row, extent):
        span = pl.ds(first_row, extent)
        for e in range(2):
            i = 2 * core + e
            part = dot(ghs[span, place(i, B)], xs[span, :], ((0,), (0,)))
            acc[0, i] = acc[0, i] + part if first_row else part

    def over_z(g, k):
        cols = place(lax.rem(z + k, 4), B)
        for e in range(2):
            net.arrived(swap[g, k, e])
            zs[g].put(k, e, acc[g, 2 * c + e, :, cols] + other[g, e, :, cols])

    def leaving(g, e, slot):
        return pltpu.make_async_remote_copy(
            src_ref=leave.at[g, e],
            dst_ref=grads_out.at[g, slot],
            send_sem=send.at[COPIES + 2 * g + e],
            recv_sem=recv.at[COPIES + 2 * g + slot],
            device_id={"x": 2 * c + e, "c": x // 2},
            device_id_type=MESH,
        )

    def staying(g, e):
        return pltpu.make_async_copy(leave.at[g, e], grads_out.at[g, e], local.at[9 + 2 * g + e])

    def to_owner(g):
        for e, value in enumerate(zs[g].finish()):
            leave[g, e] = (value.T if g == 0 else value).astype(bf16)

            @pl.when(2 * c + e != x)
            def _(e=e):
                leaving(g, e, lax.rem(x, 2)).start()

            @pl.when(2 * c + e == x)
            def _(e=e):
                staying(g, e).start()

    def collect(g):
        for e in range(2):

            @pl.when(2 * c + e != x)
            def _(e=e):
                copy = leaving(g, e, e)
                copy.wait_recv()
                copy.wait_send()

            @pl.when(2 * c + e == x)
            def _(e=e):
                staying(g, e).wait()

    def weights_in(m, k):
        net.arrived(ws[m, k])
        wz[m, k].start()
        net.start(wd[m, k, 0])

    def weights_out(m, k):
        wz[m, k].finish()
        for t in (1, 3, 2):
            net.start(wd[m, k, t])

    tasks = {"tot": totals_y, "tot2": totals_x, "res": residuals}
    for m in (1, 2):
        for k in range(3):
            tasks[f"w{m}a{k}"] = lambda m=m, k=k: weights_in(m, k)
            tasks[f"w{m}b{k}"] = wz[m, k].mid
            tasks[f"w{m}c{k}"] = lambda m=m, k=k: weights_out(m, k)
    for n in range(STEPS):
        for k in range(4):
            tasks[f"f{n}{k}"] = lambda n=n, k=k: first(n, k)
            tasks[f"s{n}{k}"] = lambda n=n, k=k: second(n, k)
            tasks[f"t{n}{k}"] = lambda n=n, k=k: third(n, k)
        named = {"gx": gx, "sh": sh, "ga": ga, "sz": sz, "gu": gu, "sg": sg, "gg": gg}
        for name, ops in named.items():
            tasks[f"{name}{n}.mid"] = ops[n].mid
        tasks[f"act{n}"] = lambda n=n: activate(n)
        tasks[f"con{n}"] = lambda n=n: control(n)
        tasks[f"hid{n}"] = lambda n=n: hidden_grad(n)
        tasks[f"sc{n}"] = lambda n=n: scale(n)

    def go1():
        out_sum(1 - c)
        give(1)

    def gi1():
        for n in range(2):
            gg[n].finish()
        for core in (1 - c, c):
            in_sum(core, 0, 2 * B)

    def gi2():
        gg[2].finish()
        in_sum(1 - c, 2 * B, B)
        give(0)

    tasks |= {"go1": go1, "go2": lambda: out_sum(c), "gi1": gi1, "gi2": gi2, "gi3": lambda: in_sum(c, 2 * B, B)}
    for g, name in enumerate("io"):
        for k in range(4):
            tasks[f"p{name}{k}"] = lambda g=g, k=k: over_z(g, k)
        tasks[f"z{name}.mid"] = zs[g].mid
        tasks[f"z{name}.fin"] = lambda g=g: to_owner(g)
        tasks[f"col{name}"] = lambda g=g: collect(g)

    assert sorted(PROGRAM) == sorted(tasks)
    for name in PROGRAM:
        with jax.named_scope(name):
            tasks[name]()
    net.drain()


def placing(row, blocks, residual, grad_in, grad_out):
    residual[...] = row[...].reshape(B)
    for t in range(2):
        grad_in[pl.ds(t * B, B), :] = blocks[0, t].astype(f32)
        grad_out[:, pl.ds(t * B, B)] = blocks[1, t].astype(f32)


def on_device(start, increments, w_in, w_out, initial):
    vmem, anywhere = pl.BlockSpec(memory_space=pltpu.VMEM), pl.BlockSpec(memory_space=pl.ANY)
    stacked = pltpu.VMEM((STEPS * B, 4 * B), bf16)
    weights = pltpu.VMEM((4, 4, 2, H, B), bf16)
    row, blocks = pl.pallas_call(
        kernel,
        out_shape=(jax.ShapeDtypeStruct((1, B), f32), jax.ShapeDtypeStruct((2, 2, B, B), bf16)),
        in_specs=[anywhere] * 4 + [pl.BlockSpec(memory_space=pltpu.SMEM)],
        out_specs=(vmem, anywhere),
        scratch_shapes=[
            pltpu.VMEM((B, B), f32),
            pltpu.VMEM((STEPS, B, B), f32),
            stacked,
            stacked,
            stacked,
            stacked,
            stacked,
            weights,
            weights,
            pltpu.VMEM((STEPS, 2, H, B), f32),
            pltpu.VMEM((9, 3, 2, H, B), bf16),
            pltpu.VMEM((9, 2, H, B), bf16),
            pltpu.VMEM((9, 2, 2, H, B), bf16),
            pltpu.VMEM((9, 4, H, B), f32),
            pltpu.VMEM((2, 4, B, 4 * B), f32),
            pltpu.VMEM((2, 2, B, 4 * B), f32),
            pltpu.VMEM((2, 3, 2, B, B), bf16),
            pltpu.VMEM((2, 2, B, B), bf16),
            pltpu.VMEM((2, 4, B, B), f32),
            pltpu.VMEM((2, 2, 2, B, B), bf16),
            pltpu.VMEM((2, 2, B, B), bf16),
            pltpu.VMEM((2, 4, 8, B), f32),
            pltpu.VMEM((1, B), f32),
            pltpu.VMEM((2, H, 128), f32),
            pltpu.VMEM((B, 128), f32),
            pltpu.SemaphoreType.DMA((COPIES + 4,)),
            pltpu.SemaphoreType.DMA((COPIES + 4,)),
            pltpu.SemaphoreType.DMA((13,)),
        ],
        compiler_params=pltpu.CompilerParams(collective_id=0, has_side_effects=True, vmem_limit_bytes=66000000),
    )(start, increments, w_in.reshape(4, 4, 2, H, B), w_out.reshape(2, H, D), initial.reshape(1))
    return pl.pallas_call(
        placing,
        out_shape=(
            jax.ShapeDtypeStruct((B,), f32),
            jax.ShapeDtypeStruct((2 * B, B), f32),
            jax.ShapeDtypeStruct((B, 2 * B), f32),
        ),
        in_specs=[vmem, vmem],
        out_specs=(vmem, vmem, vmem),
    )(row, blocks)


def solution(mesh):
    finer = Mesh(mesh.devices.reshape(4, 4, 4, 2), ("y", "x", "z", "c"))
    return jax.shard_map(
        on_device,
        mesh=finer,
        in_specs=(P(BATCH, DIM), P(None, BATCH, DIM), P(None, DIM), P(DIM, None), P()),
        out_specs=(P(BATCH), P(BATCH, DIM), P(DIM, BATCH)),
        check_vma=False,
    )
```

time: 440 us -> 121 us (0.28); the launches traced: 433 us -> 121 us
  blocking collectives: 203 us -> 0 us
  Pallas kernels: 0 us -> 120 us
  waiting for transfers between devices: 92.5 us -> 0 us
  other arithmetic: 46.3 us -> 0 us
  local copies, waits for them, and re-layouts: 45.3 us -> 0 us
  matrix products: 22.5 us -> 0 us
  between operations: 15.1 us -> 1.29 us
  starting transfers between devices: 9.04 us -> 0 us
    all_to_all x5 -> x0, blocking collectives: 148 us -> none  [a2a(): return lax.all_to_all(array, axis, split_axis=0, concat_axis=0, tiled=True)]
    pallas_call x0 -> x2, Pallas kernels: none -> 120 us  [the longest x1 118 us: on_device(): pl.pallas_call(kernel, out_shape=(jax.ShapeDtypeStruct((1, B), f32), jax....]
    all_gather x5 -> x0, waiting for transfers between devices: 58.5 us -> none  [the longest x1 31.8 us: on_device(): gg = lax.all_gather(gz, 'y')]
    all_to_all x2 -> x0, waiting for transfers between devices: 33.9 us -> none  [a2a(): return lax.all_to_all(array, axis, split_axis=0, concat_axis=0, tiled=True)]
    psum x1 -> x0, blocking collectives: 28.5 us -> none  [on_device(): both = lax.psum(jnp.stack([terms, norm]), DIM)]
    unnamed x1 -> x0, blocking collectives: 26.2 us -> none
    dot_general x5 -> x0, matrix products: 22.5 us -> none  [the longest x1 5.16 us: on_device(): gin = jnp.einsum('jrd,irh->jidh', xg, hg, preferred_element_type=f32)]
    convert_element_type x6 -> x0, other arithmetic: 21.4 us -> none  [the longest x1 7.44 us: on_device(): grads.astype(bf16)]
  transfers between devices with their start and end apart: 7 -> 0, of which waited for: 6 -> 0; matrix products, arithmetic and copies ran while one was open for 4% -> 0% of each run, Pallas kernels for 0% -> 0%
where the time goes in v3:
time: 121 us
  Pallas kernels  120 us (99%)
  between operations  1.29 us (1%)
    pallas_call x1, Pallas kernels, on_device(): pl.pallas_call(kernel, out_shape=(jax.ShapeDtypeStruct((1, B), f32), jax....  118 us

profile of v3, /device:TPU:1, one launch (start us, length us, event | category | flops | bytes accessed | tf_op | source)
XLA Modules:
  0.0 121.3 jit_solution(3165752964399917688)
XLA Ops:
  1.3 118.0 %shard_map.76 = (f32[1,256]{1,0:T(1,128)}, bf16[2,2,256,256]{3,2,1,0:T(8,128)(2,1)}) custom-call(f32[256,256]{1,0:T(8,128)} %start_in.1, f32[3,256,256]{2,1,0:T(8,128)} %inc_in.1, bf16[4,4,2,128,256]{4,3,2,1,0:T(8,128)(2,1)} %bitcast.4, bf16[2,128,4096]{2,1,0:T(8,128)(2,1)} %bitcast.5, f32[1]{0:T(128)} %bitcast.3.initial), custom_call_target="tpu_custom_call" | custom-call | tf_op jit(solution)/shard_map/pallas_call | solution.py:461
  119.3 2.0 %shard_map.77 = (f32[256]{0:T(256)}, f32[512,256]{1,0:T(8,128)}, f32[256,512]{1,0:T(8,128)}) custom-call(f32[1,256]{1,0:T(1,128)} %get-tuple-element.5.row, bf16[2,2,256,256]{3,2,1,0:T(8,128)(2,1)} %get-tuple-element.6.blocks), custom_call_target="tpu_custom_call" | custom-call | tf_op jit(solution)/shard_map/pallas_call | solution.py:498

commit v4 on v3

v4 whole, which is shorter than its diff:
```python
import math

import jax
import jax.numpy as jnp
from jax import lax
from jax.experimental import pallas as pl
from jax.experimental.pallas import tpu as pltpu
from jax.sharding import Mesh
from jax.sharding import PartitionSpec as P

D = 4096
STEPS = 3
B = 256
H = B // 2
Q = B // 4
CHAINS = 2 * STEPS
DIM = ("y", "x")
BATCH = ("z", "c")
MESH = pl.DeviceIdType.MESH
f32, bf16 = jnp.float32, jnp.bfloat16

time_step = 1.0 / 64.0
lam_coef = 50.0
noise_coef = math.sqrt(2.0)
zscale = 2.0 / math.sqrt(D)
ARRIVALS = 170
LEAVING = 48


def place(pos, extent):
    return pl.ds(pl.multiple_of(pos * extent, extent), extent)


class Net:

    def __init__(self, send, recv):
        self.send, self.recv, self.count, self.begun, self.seen = send, recv, 0, [], set()

    def slots(self, count):
        self.count += count
        assert self.count <= ARRIVALS
        return [self.recv.at[k] for k in range(self.count - count, self.count)]

    def copy(self, src, dst, device, slot=None):
        return (src, dst, device, self.slots(1)[0] if slot is None else slot)

    def made(self, copy, send):
        src, dst, device, slot = copy
        return pltpu.make_async_remote_copy(
            src_ref=src, dst_ref=dst, send_sem=send, recv_sem=slot, device_id=device, device_id_type=MESH
        )

    def start(self, copy):
        send = self.send.at[len(self.begun) % LEAVING]
        if len(self.begun) >= LEAVING:
            self.begun[len(self.begun) - LEAVING].wait_send()
        made = self.made(copy, send)
        made.start()
        self.begun.append(made)

    def arrived(self, copy):
        if id(copy) not in self.seen:
            self.seen.add(id(copy))
            self.made(copy, self.send.at[0]).wait_recv()

    def drain(self):
        for copy in self.begun[-LEAVING:]:
            copy.wait_send()


class Gather:

    def __init__(self, net, axis, view, four, slots=None):
        p = lax.axis_index(axis)
        r, l = lax.rem(p + 1, 4), lax.rem(p + 3, 4)
        self.net, self.slots = net, slots or net.slots(3)
        self.copies = [
            net.copy(view(owner, half), view(owner, half), {axis: to}, self.slots[min(k, 2)])
            for k, (owner, half, to) in enumerate(((p, 0, r), (p, 1, l), (p, 1, r), (p, 0, l), (l, 0, r), (r, 1, l)))
        ]
        self.rest = (four, four, {axis: r}, self.slots[2])

    def start(self):
        for k in range(4):
            self.net.start(self.copies[k])

    def mid(self):
        for k in range(2):
            self.net.arrived(self.copies[k])
            self.net.start(self.copies[4 + k])

    def finish(self):
        self.net.arrived(self.rest)


class Scatter:

    def __init__(self, net, axis, sent, far, near, held, slots=None):
        p = lax.axis_index(axis)
        r, l = {axis: lax.rem(p + 1, 4)}, {axis: lax.rem(p + 3, 4)}
        self.net, self.sent, self.far, self.near, self.held = net, sent, far, near, held
        self.slots = slots or net.slots(3)
        a, b, rest = self.slots
        self.copies = {
            (2, 0): net.copy(sent.at[1, 0], far.at[0], r, a),
            (2, 1): net.copy(sent.at[1, 1], far.at[1], l, b),
            (1, 1): net.copy(sent.at[0, 1], near.at[0, 1], r, rest),
            (3, 0): net.copy(sent.at[2, 0], near.at[1, 0], l, rest),
            (1, 0): net.copy(sent.at[0, 0], near.at[0, 0], r, rest),
            (3, 1): net.copy(sent.at[2, 1], near.at[1, 1], l, rest),
        }
        self.rest = (near, near, r, rest)

    def put(self, k, half, value):
        if (k, half) in ((2, 0), (2, 1), (1, 1), (3, 0)):
            self.sent[k - 1, half] = value.astype(bf16)
            self.net.start(self.copies[k, half])
        else:
            self.held[{0: half, 1: 2, 3: 3}[k]] = value

    def mid(self):
        for side, key in enumerate(((1, 0), (3, 1))):
            self.net.arrived(self.copies[2, side])
            k, half = key
            self.sent[k - 1, half] = (self.held[2 + side] + self.far[side].astype(f32)).astype(bf16)
            self.net.start(self.copies[key])

    def finish(self):
        self.net.arrived(self.rest)
        near = self.near
        return [self.held[half] + near[0, half].astype(f32) + near[1, half].astype(f32) for half in range(2)]


ORDER = (2, 1, 3, 0)
PROGRAM = [
    "w1a2", "gx0.mid", "w1a1", "w1a0", "w1b1", "w1b2", "gx2.mid", "gx3.mid", "w1b0", "w2a2", "w1c1", "gx1.mid",
    "gx5.mid", "w2a1", "gx4.mid", "w1c2", "f22", "w1c0", "f32", "f20", "w2b2", "f02", "f21", "f12", "f10", "w2a0",
    "f23", "f40", "sh2.mid", "f31", "f33", "w2b1", "sh3.mid", "f01", "f03", "f50", "f00", "w2b0", "sh0.mid", "w2c2",
    "f30", "act2", "w2c1", "act3", "ga2.mid", "act0", "w2c0", "ga3.mid", "f11", "f13", "sh1.mid", "s22", "s21", "s23",
    "ga0.mid", "f42", "f52", "f43", "f41", "s32", "s31", "sz2.mid", "act1", "s33", "s20", "s02", "s01", "sh4.mid",
    "f51", "sz3.mid", "f53", "s03", "sh5.mid", "con2", "s30", "ga1.mid", "s00", "sz0.mid", "act4", "con3", "act5",
    "gu2.mid", "s12", "con0", "ga4.mid", "s11", "gu3.mid", "s13", "ga5.mid", "sz1.mid", "t22", "s42", "s41",
    "gu0.mid", "s43", "s10", "s52", "s40", "con1", "t32", "sz4.mid", "t31", "s53", "t21", "s51", "s50", "t33",
    "sz5.mid", "t02", "t23", "gu1.mid", "sg2.mid", "t00", "t20", "con4", "t03", "t01", "con5", "t30", "t12",
    "sg3.mid", "tot", "sg0.mid", "t13", "gu4.mid", "t11", "gu5.mid", "sg1.mid", "tot2", "t42", "t43", "t41", "t53",
    "t51", "t40", "t52", "sg4.mid", "res", "hid0", "hid2", "resp", "sc5", "sc4", "sc3", "sc2", "hid3", "sc0", "sc1",
    "go1", "hid4", "go0", "t10", "po11", "hid1", "t50", "gg3.mid", "po01", "po02", "sg5.mid", "gg0.mid", "gg2.mid",
    "po13", "gg4.mid", "po03", "gs3", "gg1.mid", "po12", "hid5", "gs0", "po00", "gs2", "gs4", "gs1", "gg5.mid", "gi0",
    "zo0.mid", "zo1.mid", "gs5", "gi1", "gj0", "gj1", "pi02", "po10", "pi12", "pi01", "pi00", "pi03", "zo1.fin",
    "zo0.fin", "zi0.mid", "pi11", "pi13", "pi10", "zi1.mid", "zi0.fin", "zi1.fin", "colo", "coli",
]


def dot(a, b, dims):
    return lax.dot_general(a, b, (dims, ((), ())), preferred_element_type=f32)


def kernel(
    start_in, inc_in, w_in, w_out, initial_in,
    res_out, grads_out,
    start, inc, xs, us, acts, scaled, ghs, w1, w2, slopes,
    sent, far, near, held, acc, zsent, zfar, zheld, znear,
    leave, totals, nrow, folded, resrow, rowres, give1, give2, initial, send, recv, local,
):
    y, x, z, c = (lax.axis_index(a) for a in ("y", "x", "z", "c"))

    barrier = pltpu.get_barrier_semaphore()
    peers = [{a: lax.rem(i + k, 4)} for a, i in (("x", x), ("y", y)) for k in (1, 2, 3)]
    peers += [{"z": lax.rem(z + k, 4)} for k in (1, 3)]
    peers += [{"c": 1 - c}] + [{"x": lax.rem(x + k, 4), "c": 1 - c} for k in (1, 2, 3)]
    for peer in peers:
        pl.semaphore_signal(barrier, inc=1, device_id=peer, device_id_type=MESH)

    fetch = [pltpu.make_async_copy(start_in, start, local.at[0])]
    fetch += [pltpu.make_async_copy(inc_in.at[n], inc.at[n], local.at[1 + n]) for n in range(STEPS)]
    own1 = [pltpu.make_async_copy(w_in.at[:, x], w1.at[x], local.at[4])]
    own2 = []
    for j in range(4):
        cols = pl.ds(pl.multiple_of(1024 * j + x * B, B), B)
        own2.append(pltpu.make_async_copy(w_out.at[:, :, cols], w2.at[j, x], local.at[5 + j]))
    gift1 = pltpu.make_async_copy(w_in.at[z, :, c], give1, local.at[9])
    gift2 = pltpu.make_async_copy(w_out.at[c, :, pl.ds(pl.multiple_of(z * 1024, 1024), 1024)], give2, local.at[10])
    scalar = pltpu.make_async_copy(initial_in, initial, local.at[11])
    for copy in [gift1] + fetch + [gift2] + own1 + own2 + [scalar]:
        copy.start()

    net = Net(send, recv)
    partner = {"c": 1 - c}

    def states_of(ref, n):
        return lambda owner, half: ref.at[n // 2, c, pl.ds(n % 2 * H + half * Q, Q), place(owner, B)]

    def hidden_of(ref, n):
        return lambda owner, half: ref.at[owner, n // 2, c, pl.ds(n % 2 * H + half * Q, Q)]

    def span(n):
        return pl.ds(n % 2 * H, H)

    def quarters(n):
        return [(half, pl.ds(n % 2 * H + half * Q, Q)) for half in range(2)]

    def piece(m, i, j):
        return w1.at[i, j, c] if m == 1 else w2.at[j, i, c]

    def quarter(m, i):
        return lambda owner, half: piece(m, i, owner).at[pl.ds(half * 64, 64)]

    four = acts.at[0, 0, 0]
    gx = [Gather(net, "y", states_of(xs, n), four) for n in range(CHAINS)]
    others = [lax.rem(x + k, 4) for k in (1, 2, 3)]
    froms = [lax.rem(x + 4 - k, 4) for k in (1, 2, 3)]
    ws, wz, wd = {}, {}, {}
    for m in (1, 2):
        for k, i in enumerate(others):
            src = give1.at[i] if m == 1 else give2.at[:, place(i, B)]
            ws[m, k] = net.copy(src, piece(m, x, z), {"x": i})
        for k, i in enumerate(froms):
            wz[m, k] = Gather(net, "z", quarter(m, i), four)
            slot = net.slots(1)[0]
            for t in range(4):
                mine = piece(m, i, lax.rem(z + t, 4))
                wd[m, k, t] = net.copy(mine, mine, {"c": 1 - c}, slot)
            whole = w1.at[i, :, c] if m == 1 else w2.at[:, i, c]
            wd[m, k] = (whole, whole, {"c": 1 - c}, slot)

    def scatter(axis, k, slots=None):
        return Scatter(net, axis, sent.at[k], far.at[k], near.at[k], held.at[k], slots)

    sh = [scatter("x", n) for n in range(CHAINS)]
    sz = [scatter("y", CHAINS + n) for n in range(CHAINS)]
    sg = [scatter("x", 2 * CHAINS + n, sh[n].slots) for n in range(CHAINS)]
    ga = [Gather(net, "x", hidden_of(acts, n), four) for n in range(CHAINS)]
    gu = [Gather(net, "y", states_of(us, n), four, gx[n].slots) for n in range(CHAINS)]
    gg = [Gather(net, "x", hidden_of(ghs, n), four, ga[n].slots) for n in range(CHAINS)]
    over_y, over_x = net.slots(2)
    ty = [net.copy(totals.at[0, y], totals.at[0, y], {"y": lax.rem(y + k, 4)}, over_y) for k in (1, 2, 3)]
    tx = [net.copy(totals.at[1, x], totals.at[1, x], {"x": lax.rem(x + k, 4)}, over_x) for k in (1, 2, 3)]
    three = totals.at[0, pl.ds(0, 3)]
    ty_all, tx_all = (three, three, partner, over_y), (three, three, partner, over_x)
    def to_partner(ref):
        return net.copy(ref, ref, partner)

    def pair_to_partner(ref, n):
        slot = net.slots(1)[0]
        pair = [ref.at[2 * (1 - c) + e, n // 2, c, span(n)] for e in range(2)]
        both = ref.at[pl.ds(2 * c, 2), n // 2, 1 - c, span(n)]
        return [(p, p, partner, slot) for p in pair], (both, both, partner, slot)

    dx = [[to_partner(xs.at[n // 2, c, span(n)])] for n in range(CHAINS)]
    du = [[to_partner(us.at[n // 2, c, span(n)])] for n in range(CHAINS)]
    da = [pair_to_partner(acts, n) for n in range(CHAINS)]
    dg = [pair_to_partner(ghs, n) for n in range(CHAINS)]
    dr = to_partner(resrow.at[c])
    zs = [
        [Scatter(net, "z", zsent.at[g, r], zfar.at[g, r], znear.at[g, r], zheld.at[g, r]) for r in range(2)] for g in range(2)
    ]

    def per_path(t):
        return jnp.sum(t.T, axis=0, keepdims=True)

    with jax.named_scope("barrier"):
        pl.semaphore_wait(barrier, len(peers))
    gift1.wait()
    for k in (1, 0, 2):
        net.start(ws[1, k])
    fetch[0].wait()
    state = start[...]
    for n in range(STEPS):
        xs[n, c, :, place(y, B)] = state.astype(bf16)
        gx[2 * n].start()
        gx[2 * n + 1].start()
        if n == 0:
            gift2.wait()
            for k in (1, 0, 2):
                net.start(ws[2, k])
        fetch[1 + n].wait()
        state = state + noise_coef * inc[n]
    norm = state * state
    nrow[...] = per_path(norm[:, :128] + norm[:, 128:])
    scalar.wait()

    def put_both(scatter_sum, k, part):
        for half in range(2):
            scatter_sum.put(k, half, part[half * Q : half * Q + Q])

    ready = set()

    def share(key, copies):
        if key not in ready:
            ready.add(key)
            for copy in copies:
                net.start(copy)

    def wait_once(copies):
        for copy in copies:
            if id(copy) not in ready:
                ready.add(id(copy))
                copy.wait()

    def weights(m, k):
        net.arrived(wd[m, k])

    def first(n, k):
        gx[n].finish()
        if k:
            weights(1, 3 - k)
        else:
            wait_once(own1)
        w = w1[lax.rem(x + k, 4)].reshape(4 * B, B)
        put_both(sh[n], k, dot(xs[n // 2, c, span(n)], w, ((1,), (0,))))
        share(("x", n), dx[n])

    def second(n, k):
        ga[n].finish()
        for e in range(3):
            weights(2, e)
        wait_once(own2)
        j = lax.rem(y + k, 4)
        part = None
        for i in range(4):
            term = dot(acts[i, n // 2, c, span(n)], w2[j, i].reshape(B, B), ((1,), (0,)))
            part = term if part is None else part + term
        put_both(sz[n], k, part)
        share(("a", n), da[n][0])

    def third(n, k):
        gu[n].finish()
        i = lax.rem(x + k, 4)
        part = None
        for j in range(4):
            term = dot(us[n // 2, c, span(n), pl.ds(j * B, B)], w2[j, i].reshape(B, B), ((1,), (1,)))
            part = term if part is None else part + term
        put_both(sg[n], k, part)
        share(("u", n), du[n])

    def activate(n):
        for (half, at), h in zip(quarters(n), sh[n].finish()):
            sig = jax.nn.sigmoid(h)
            acts[x, n // 2, c, at] = (h * sig).astype(bf16)
            slopes[n, half] = sig * (1.0 + h * (1.0 - sig))
        ga[n].start()

    begun = set()

    def control(n):
        for (half, at), total in zip(quarters(n), sz[n].finish()):
            zval = zscale * total
            dw = inc[n // 2, at, :]
            us[n // 2, c, at, place(y, B)] = (zscale * (lam_coef * time_step * zval + dw)).astype(bf16)
            term = 0.5 * lam_coef * time_step * zval * zval + zval * dw
            term = term[:, :128] + term[:, 128:]
            folded[at, :] = folded[at, :] + term if n % 2 in begun else term
        begun.add(n % 2)
        gu[n].start()

    def hidden_grad(n):
        for (half, at), g in zip(quarters(n), sg[n].finish()):
            r = rowres[c, at, :]
            r = jnp.concatenate([r, r], axis=1)
            ghs[x, n // 2, c, at] = (r * g * slopes[n, half]).astype(bf16)
        gg[n].start()

    def totals_y():
        y_row = per_path(folded[...])
        totals[0, y] = jnp.concatenate([y_row, nrow[...], jnp.zeros((6, B), f32)], axis=0)
        for copy in ty:
            net.start(copy)

    def totals_x():
        net.arrived(ty_all)
        totals[1, x] = totals[0, 0] + totals[0, 1] + totals[0, 2] + totals[0, 3]
        for copy in tx:
            net.start(copy)

    kept_row = pltpu.make_async_copy(resrow.at[c], res_out, local.at[12])

    def residuals():
        net.arrived(tx_all)
        both = totals[1, 0] + totals[1, 1] + totals[1, 2] + totals[1, 3]
        residual = initial[0] + both[0:1] - jnp.log((1.0 + both[1:2]) * 0.5)
        resrow[c] = jnp.broadcast_to(residual, (8, B))
        net.start(dr)
        kept_row.start()
        rowres[c] = jnp.broadcast_to(residual, (128, B)).T

    def partner_residuals():
        net.arrived(dr)
        rowres[1 - c] = jnp.broadcast_to(resrow[1 - c, 0:1], (128, B)).T

    def scale(n):
        net.arrived(da[n][1])
        for e in range(2):
            for core in range(2):
                for k in range(2):
                    lanes = pl.ds(k * 128, 128)
                    a = acts[2 * c + e, n // 2, core, span(n), lanes].astype(f32)
                    scaled[e, n // 2, core, span(n), lanes] = (a * rowres[core, span(n)]).astype(bf16)

    def out_sum(e):
        for n in range(CHAINS):
            gu[n].finish()
            for copy in du[n]:
                net.arrived(copy)
        every = STEPS * 2 * B
        acc[1, e] = dot(scaled[e].reshape(every, B), us[...].reshape(every, 4 * B), ((0,), (0,)))

    def give(n):
        gg[n].finish()
        for copy in dg[n][0]:
            net.start(copy)

    def of_chain(e, n):
        for copy in dx[n] + [dg[n][1]]:
            net.arrived(copy)
        g = ghs[2 * c + e, n // 2, :, span(n)].reshape(B, B)
        return dot(g, xs[n // 2, :, span(n)].reshape(B, 4 * B), ((0,), (0,)))

    def in_sum(e):
        for n in range(4):
            for copy in dx[n] + [dg[n][1]]:
                net.arrived(copy)
        g = ghs[2 * c + e, pl.ds(0, 2)].reshape(4 * B, B)
        acc[0, e] = dot(g, xs[pl.ds(0, 2)].reshape(4 * B, 4 * B), ((0,), (0,))) + of_chain(e, 4)

    def in_last(e):
        acc[0, e] = acc[0, e] + of_chain(e, 5)

    def over_z(g, r, k):
        cols = place(lax.rem(z + k, 4), B)
        for e in range(2):
            zs[g][r].put(k, e, acc[g, e, pl.ds(r * H, H), cols])

    def leaving(g, r, e, slot):
        rows = pl.ds(r * H, H)
        k = 4 * g + 2 * r
        return pltpu.make_async_remote_copy(
            src_ref=leave.at[g, e, rows],
            dst_ref=grads_out.at[g, slot, rows],
            send_sem=send.at[LEAVING + k + e],
            recv_sem=recv.at[ARRIVALS + k + slot],
            device_id={"x": 2 * c + e, "c": x // 2},
            device_id_type=MESH,
        )

    def staying(g, r, e):
        rows = pl.ds(r * H, H)
        return pltpu.make_async_copy(leave.at[g, e, rows], grads_out.at[g, e, rows], local.at[13 + 4 * g + 2 * r + e])

    def to_owner(g, r):
        for e, value in enumerate(zs[g][r].finish()):
            leave[g, e, pl.ds(r * H, H)] = value.astype(bf16)

            @pl.when(2 * c + e != x)
            def _(e=e):
                leaving(g, r, e, lax.rem(x, 2)).start()

            @pl.when(2 * c + e == x)
            def _(e=e):
                staying(g, r, e).start()

    def collect(g):
        for r in range(2):
            for e in range(2):

                @pl.when(2 * c + e != x)
                def _(r=r, e=e):
                    copy = leaving(g, r, e, e)
                    copy.wait_recv()
                    copy.wait_send()

                @pl.when(2 * c + e == x)
                def _(r=r, e=e):
                    staying(g, r, e).wait()

    def weights_in(m, k):
        net.arrived(ws[m, k])
        wz[m, k].start()
        net.start(wd[m, k, 0])

    def weights_out(m, k):
        wz[m, k].finish()
        for t in (1, 3, 2):
            net.start(wd[m, k, t])

    tasks = {"tot": totals_y, "tot2": totals_x, "res": residuals, "resp": partner_residuals}
    for m in (1, 2):
        for k in range(3):
            tasks[f"w{m}a{k}"] = lambda m=m, k=k: weights_in(m, k)
            tasks[f"w{m}b{k}"] = wz[m, k].mid
            tasks[f"w{m}c{k}"] = lambda m=m, k=k: weights_out(m, k)
    for n in range(CHAINS):
        for k in range(4):
            tasks[f"f{n}{k}"] = lambda n=n, k=k: first(n, k)
            tasks[f"s{n}{k}"] = lambda n=n, k=k: second(n, k)
            tasks[f"t{n}{k}"] = lambda n=n, k=k: third(n, k)
        named = {"gx": gx, "sh": sh, "ga": ga, "sz": sz, "gu": gu, "sg": sg, "gg": gg}
        for name, ops in named.items():
            tasks[f"{name}{n}.mid"] = ops[n].mid
        tasks[f"act{n}"] = lambda n=n: activate(n)
        tasks[f"con{n}"] = lambda n=n: control(n)
        tasks[f"hid{n}"] = lambda n=n: hidden_grad(n)
        tasks[f"sc{n}"] = lambda n=n: scale(n)
        tasks[f"gs{n}"] = lambda n=n: give(n)

    for e in range(2):
        tasks[f"go{e}"] = lambda e=e: out_sum(e)
        tasks[f"gi{e}"] = lambda e=e: in_sum(e)
        tasks[f"gj{e}"] = lambda e=e: in_last(e)
    for g, name in enumerate("io"):
        for r in range(2):
            for k in range(4):
                tasks[f"p{name}{r}{k}"] = lambda g=g, r=r, k=k: over_z(g, r, k)
            tasks[f"z{name}{r}.mid"] = zs[g][r].mid
            tasks[f"z{name}{r}.fin"] = lambda g=g, r=r: to_owner(g, r)
        tasks[f"col{name}"] = lambda g=g: collect(g)

    assert sorted(PROGRAM) == sorted(tasks)
    for name in PROGRAM:
        with jax.named_scope(name):
            tasks[name]()
    kept_row.wait()
    net.drain()


def placing(row, blocks, residual, grad_in, grad_out):
    residual[...] = row[0:1].reshape(B)
    for t in range(2):
        grad_in[pl.ds(t * B, B), :] = blocks[0, t].astype(f32).T
        grad_out[:, pl.ds(t * B, B)] = blocks[1, t].astype(f32)


def on_device(start, increments, w_in, w_out, initial):
    vmem, anywhere = pl.BlockSpec(memory_space=pltpu.VMEM), pl.BlockSpec(memory_space=pl.ANY)
    states = pltpu.VMEM((STEPS, 2, B, 4 * B), bf16)
    hidden = pltpu.VMEM((4, STEPS, 2, B, B), bf16)
    weights = pltpu.VMEM((4, 4, 2, H, B), bf16)
    row, blocks = pl.pallas_call(
        kernel,
        out_shape=(jax.ShapeDtypeStruct((8, B), f32), jax.ShapeDtypeStruct((2, 2, B, B), bf16)),
        in_specs=[anywhere] * 5,
        out_specs=(anywhere, anywhere),
        scratch_shapes=[
            pltpu.VMEM((B, B), f32),
            pltpu.VMEM((STEPS, B, B), f32),
            states,
            states,
            hidden,
            pltpu.VMEM((2, STEPS, 2, B, B), bf16),
            hidden,
            weights,
            weights,
            pltpu.VMEM((CHAINS, 2, Q, B), f32),
            pltpu.VMEM((3 * CHAINS, 3, 2, Q, B), bf16),
            pltpu.VMEM((3 * CHAINS, 2, Q, B), bf16),
            pltpu.VMEM((3 * CHAINS, 2, 2, Q, B), bf16),
            pltpu.VMEM((3 * CHAINS, 4, Q, B), f32),
            pltpu.VMEM((2, 2, B, 4 * B), f32),
            pltpu.VMEM((2, 2, 3, 2, H, B), bf16),
            pltpu.VMEM((2, 2, 2, H, B), bf16),
            pltpu.VMEM((2, 2, 4, H, B), f32),
            pltpu.VMEM((2, 2, 2, 2, H, B), bf16),
            pltpu.VMEM((2, 2, B, B), bf16),
            pltpu.VMEM((2, 4, 8, B), f32),
            pltpu.VMEM((1, B), f32),
            pltpu.VMEM((B, 128), f32),
            pltpu.VMEM((2, 8, B), f32),
            pltpu.VMEM((2, B, 128), f32),
            pltpu.VMEM((4, H, B), bf16),
            pltpu.VMEM((H, 4 * B), bf16),
            pltpu.SMEM((1,), f32),
            pltpu.SemaphoreType.DMA((LEAVING + 8,)),
            pltpu.SemaphoreType.DMA((ARRIVALS + 8,)),
            pltpu.SemaphoreType.DMA((21,)),
        ],
        compiler_params=pltpu.CompilerParams(collective_id=0, has_side_effects=True, vmem_limit_bytes=66000000),
    )(start, increments, w_in.reshape(4, 4, 2, H, B), w_out.reshape(2, H, D), initial.reshape(1))
    return pl.pallas_call(
        placing,
        out_shape=(
            jax.ShapeDtypeStruct((B,), f32),
            jax.ShapeDtypeStruct((2 * B, B), f32),
            jax.ShapeDtypeStruct((B, 2 * B), f32),
        ),
        in_specs=[vmem, vmem],
        out_specs=(vmem, vmem, vmem),
    )(row, blocks)


def solution(mesh):
    finer = Mesh(mesh.devices.reshape(4, 4, 4, 2), ("y", "x", "z", "c"))
    return jax.shard_map(
        on_device,
        mesh=finer,
        in_specs=(P(BATCH, DIM), P(None, BATCH, DIM), P(None, DIM), P(DIM, None), P()),
        out_specs=(P(BATCH), P(BATCH, DIM), P(DIM, BATCH)),
        check_vma=False,
    )
```

time: 121 us -> 116 us (0.959)
  Pallas kernels: 120 us -> 114 us
    pallas_call x1, Pallas kernels: 118 us -> 112 us  [on_device(): pl.pallas_call(kernel, out_shape=(jax.ShapeDtypeStruct((8, B), f32), jax....]
where the time goes in v4:
time: 116 us
  Pallas kernels  114 us (98%)
  between operations  1.29 us (1%)
    pallas_call x1, Pallas kernels, on_device(): pl.pallas_call(kernel, out_shape=(jax.ShapeDtypeStruct((8, B), f32), jax....  112 us

profile of v4, /device:TPU:1, one launch (start us, length us, event | category | flops | bytes accessed | tf_op | source)
XLA Modules:
  0.0 115.5 jit_solution(16873574895752319678)
XLA Ops:
  1.3 112.1 %shard_map.76 = (f32[8,256]{1,0:T(8,128)}, bf16[2,2,256,256]{3,2,1,0:T(8,128)(2,1)}) custom-call(f32[256,256]{1,0:T(8,128)} %start_in.1, f32[3,256,256]{2,1,0:T(8,128)} %inc_in.1, bf16[4,4,2,128,256]{4,3,2,1,0:T(8,128)(2,1)} %bitcast.4, bf16[2,128,4096]{2,1,0:T(8,128)(2,1)} %bitcast.5, f32[1]{0:T(128)} %bitcast.3.initial_in), custom_call_target="tpu_custom_call" | custom-call | tf_op jit(solution)/shard_map/pallas_call | solution.py:537
  113.3 2.2 %shard_map.77 = (f32[256]{0:T(256)}, f32[512,256]{1,0:T(8,128)}, f32[256,512]{1,0:T(8,128)}) custom-call(f32[8,256]{1,0:T(8,128)} %get-tuple-element.5.row, bf16[2,2,256,256]{3,2,1,0:T(8,128)(2,1)} %get-tuple-element.6.blocks), custom_call_target="tpu_custom_call" | custom-call | tf_op jit(solution)/shard_map/pallas_call | solution.py:577

commit v5 on v4

--- a/solution.py
+++ b/solution.py
@@ -133,21 +133,21 @@
 
 ORDER = (2, 1, 3, 0)
 PROGRAM = [
-    "w1a2", "gx0.mid", "w1a1", "w1a0", "w1b1", "w1b2", "gx2.mid", "gx3.mid", "w1b0", "w2a2", "w1c1", "gx1.mid",
-    "gx5.mid", "w2a1", "gx4.mid", "w1c2", "f22", "w1c0", "f32", "f20", "w2b2", "f02", "f21", "f12", "f10", "w2a0",
-    "f23", "f40", "sh2.mid", "f31", "f33", "w2b1", "sh3.mid", "f01", "f03", "f50", "f00", "w2b0", "sh0.mid", "w2c2",
-    "f30", "act2", "w2c1", "act3", "ga2.mid", "act0", "w2c0", "ga3.mid", "f11", "f13", "sh1.mid", "s22", "s21", "s23",
-    "ga0.mid", "f42", "f52", "f43", "f41", "s32", "s31", "sz2.mid", "act1", "s33", "s20", "s02", "s01", "sh4.mid",
-    "f51", "sz3.mid", "f53", "s03", "sh5.mid", "con2", "s30", "ga1.mid", "s00", "sz0.mid", "act4", "con3", "act5",
-    "gu2.mid", "s12", "con0", "ga4.mid", "s11", "gu3.mid", "s13", "ga5.mid", "sz1.mid", "t22", "s42", "s41",
-    "gu0.mid", "s43", "s10", "s52", "s40", "con1", "t32", "sz4.mid", "t31", "s53", "t21", "s51", "s50", "t33",
-    "sz5.mid", "t02", "t23", "gu1.mid", "sg2.mid", "t00", "t20", "con4", "t03", "t01", "con5", "t30", "t12",
-    "sg3.mid", "tot", "sg0.mid", "t13", "gu4.mid", "t11", "gu5.mid", "sg1.mid", "tot2", "t42", "t43", "t41", "t53",
-    "t51", "t40", "t52", "sg4.mid", "res", "hid0", "hid2", "resp", "sc5", "sc4", "sc3", "sc2", "hid3", "sc0", "sc1",
-    "go1", "hid4", "go0", "t10", "po11", "hid1", "t50", "gg3.mid", "po01", "po02", "sg5.mid", "gg0.mid", "gg2.mid",
-    "po13", "gg4.mid", "po03", "gs3", "gg1.mid", "po12", "hid5", "gs0", "po00", "gs2", "gs4", "gs1", "gg5.mid", "gi0",
-    "zo0.mid", "zo1.mid", "gs5", "gi1", "gj0", "gj1", "pi02", "po10", "pi12", "pi01", "pi00", "pi03", "zo1.fin",
-    "zo0.fin", "zi0.mid", "pi11", "pi13", "pi10", "zi1.mid", "zi0.fin", "zi1.fin", "colo", "coli",
+    "w1a2", "w1a1", "w1a0", "w1b2", "gx3.mid", "w1b1", "gx4.mid", "w1b0", "w1c2", "gx2.mid", "gx5.mid", "w2a0",
+    "w1c1", "f32", "w2a2", "w2a1", "f42", "w1c0", "f22", "f52", "f21", "f23", "w2b0", "f43", "gx0.mid", "f41",
+    "gx1.mid", "f30", "sh4.mid", "sh2.mid", "w2b2", "f40", "f53", "f51", "sh5.mid", "w2c0", "w2b1", "f31", "f33",
+    "act4", "w2c2", "f00", "f50", "f20", "act2", "w2c1", "ga4.mid", "act5", "ga2.mid", "f12", "sh3.mid", "s42", "s43",
+    "f02", "s41", "ga5.mid", "f11", "f13", "s22", "sh1.mid", "s21", "s23", "sz4.mid", "act3", "f03", "f01", "s20",
+    "sh0.mid", "s52", "f10", "sz2.mid", "s51", "s53", "act1", "s40", "con4", "s50", "ga3.mid", "sz5.mid", "act0",
+    "con2", "gu4.mid", "ga1.mid", "s33", "s31", "s32", "ga0.mid", "s30", "con5", "gu2.mid", "s12", "t42", "s02",
+    "gu5.mid", "s01", "s00", "s03", "t43", "sz3.mid", "s11", "s13", "s10", "sz1.mid", "t21", "sz0.mid", "t53", "t40",
+    "t52", "t22", "con3", "t51", "con1", "t23", "t41", "con0", "sg4.mid", "t20", "tot", "sg5.mid", "gu3.mid", "t50",
+    "sg2.mid", "gu1.mid", "gu0.mid", "tot2", "t32", "t33", "t31", "t12", "t11", "t13", "t02", "t01", "sg3.mid", "res",
+    "hid5", "t03", "t10", "hid2", "sg0.mid", "sg1.mid", "resp", "sc1", "sc3", "sc4", "sc2", "sc0", "sc5", "hid4",
+    "gg5.mid", "go0", "t30", "go1", "po10", "hid3", "po02", "t00", "po03", "po01", "po12", "hid0", "hid1", "gg4.mid",
+    "po00", "zo0.mid", "po13", "gg2.mid", "gg3.mid", "gg0.mid", "po11", "gg1.mid", "zo1.mid", "gs2", "gs3", "gs4",
+    "gs5", "gs0", "gs1", "gi1", "gi0", "gj1", "gj0", "pi12", "pi13", "pi11", "zo0.fin", "pi02", "zo1.fin", "pi10",
+    "zi1.mid", "pi03", "pi01", "zi0.mid", "zi1.fin", "colo", "pi00", "zi0.fin", "coli",
 ]
 
 

time: 116 us -> 113 us (0.974)
  Pallas kernels: 114 us -> 112 us
    pallas_call x1, Pallas kernels: 112 us -> 110 us  [on_device(): pl.pallas_call(kernel, out_shape=(jax.ShapeDtypeStruct((8, B), f32), jax....]
where the time goes in v5:
time: 113 us
  Pallas kernels  112 us (99%)
  between operations  1.29 us (1%)
    pallas_call x1, Pallas kernels, on_device(): pl.pallas_call(kernel, out_shape=(jax.ShapeDtypeStruct((8, B), f32), jax....  110 us

profile of v5, /device:TPU:1, one launch (start us, length us, event | category | flops | bytes accessed | tf_op | source)
XLA Modules:
  0.0 113.1 jit_solution(16492507656231661211)
XLA Ops:
  1.3 109.6 %shard_map.76 = (f32[8,256]{1,0:T(8,128)}, bf16[2,2,256,256]{3,2,1,0:T(8,128)(2,1)}) custom-call(f32[256,256]{1,0:T(8,128)} %start_in.1, f32[3,256,256]{2,1,0:T(8,128)} %inc_in.1, bf16[4,4,2,128,256]{4,3,2,1,0:T(8,128)(2,1)} %bitcast.4, bf16[2,128,4096]{2,1,0:T(8,128)(2,1)} %bitcast.5, f32[1]{0:T(128)} %bitcast.3.initial_in), custom_call_target="tpu_custom_call" | custom-call | tf_op jit(solution)/shard_map/pallas_call | solution.py:537
  110.9 2.2 %shard_map.77 = (f32[256]{0:T(256)}, f32[512,256]{1,0:T(8,128)}, f32[256,512]{1,0:T(8,128)}) custom-call(f32[8,256]{1,0:T(8,128)} %get-tuple-element.5.row, bf16[2,2,256,256]{3,2,1,0:T(8,128)(2,1)} %get-tuple-element.6.blocks), custom_call_target="tpu_custom_call" | custom-call | tf_op jit(solution)/shard_map/pallas_call | solution.py:577

commit v6 on v5

--- a/solution.py
+++ b/solution.py
@@ -133,21 +133,21 @@
 
 ORDER = (2, 1, 3, 0)
 PROGRAM = [
-    "w1a2", "w1a1", "w1a0", "w1b2", "gx3.mid", "w1b1", "gx4.mid", "w1b0", "w1c2", "gx2.mid", "gx5.mid", "w2a0",
-    "w1c1", "f32", "w2a2", "w2a1", "f42", "w1c0", "f22", "f52", "f21", "f23", "w2b0", "f43", "gx0.mid", "f41",
-    "gx1.mid", "f30", "sh4.mid", "sh2.mid", "w2b2", "f40", "f53", "f51", "sh5.mid", "w2c0", "w2b1", "f31", "f33",
-    "act4", "w2c2", "f00", "f50", "f20", "act2", "w2c1", "ga4.mid", "act5", "ga2.mid", "f12", "sh3.mid", "s42", "s43",
-    "f02", "s41", "ga5.mid", "f11", "f13", "s22", "sh1.mid", "s21", "s23", "sz4.mid", "act3", "f03", "f01", "s20",
-    "sh0.mid", "s52", "f10", "sz2.mid", "s51", "s53", "act1", "s40", "con4", "s50", "ga3.mid", "sz5.mid", "act0",
-    "con2", "gu4.mid", "ga1.mid", "s33", "s31", "s32", "ga0.mid", "s30", "con5", "gu2.mid", "s12", "t42", "s02",
-    "gu5.mid", "s01", "s00", "s03", "t43", "sz3.mid", "s11", "s13", "s10", "sz1.mid", "t21", "sz0.mid", "t53", "t40",
-    "t52", "t22", "con3", "t51", "con1", "t23", "t41", "con0", "sg4.mid", "t20", "tot", "sg5.mid", "gu3.mid", "t50",
-    "sg2.mid", "gu1.mid", "gu0.mid", "tot2", "t32", "t33", "t31", "t12", "t11", "t13", "t02", "t01", "sg3.mid", "res",
-    "hid5", "t03", "t10", "hid2", "sg0.mid", "sg1.mid", "resp", "sc1", "sc3", "sc4", "sc2", "sc0", "sc5", "hid4",
-    "gg5.mid", "go0", "t30", "go1", "po10", "hid3", "po02", "t00", "po03", "po01", "po12", "hid0", "hid1", "gg4.mid",
-    "po00", "zo0.mid", "po13", "gg2.mid", "gg3.mid", "gg0.mid", "po11", "gg1.mid", "zo1.mid", "gs2", "gs3", "gs4",
-    "gs5", "gs0", "gs1", "gi1", "gi0", "gj1", "gj0", "pi12", "pi13", "pi11", "zo0.fin", "pi02", "zo1.fin", "pi10",
-    "zi1.mid", "pi03", "pi01", "zi0.mid", "zi1.fin", "colo", "pi00", "zi0.fin", "coli",
+    "w1a2", "w1a1", "gx0.mid", "w1b2", "gx1.mid", "w1c2", "w1b0", "w1a0", "gx3.mid", "w1b1", "w1c1", "w2a1", "f01",
+    "w2a0", "f02", "w1c0", "f32", "gx2.mid", "f30", "f11", "f12", "gx5.mid", "f00", "f03", "f31", "w2a2", "f33",
+    "sh0.mid", "w2b1", "sh3.mid", "f13", "gx4.mid", "f22", "w2b0", "sh1.mid", "w2b2", "act0", "w2c1", "f20", "f10",
+    "act3", "f21", "w2c0", "ga0.mid", "act1", "w2c2", "ga3.mid", "f23", "sh2.mid", "f50", "s02", "s01", "f52", "s03",
+    "ga1.mid", "f51", "f42", "s32", "act2", "s33", "s00", "sz0.mid", "f53", "s31", "sh5.mid", "f41", "s12", "f43",
+    "sz3.mid", "sh4.mid", "s11", "ga2.mid", "s13", "con0", "s10", "act5", "sz1.mid", "f40", "s30", "con3", "act4",
+    "s22", "gu0.mid", "ga5.mid", "con1", "s21", "s23", "ga4.mid", "sz2.mid", "gu3.mid", "s52", "gu1.mid", "s42",
+    "s20", "con2", "s53", "s51", "t32", "t03", "sz5.mid", "s41", "s43", "sz4.mid", "t12", "t31", "s50", "gu2.mid",
+    "t11", "t02", "t13", "t33", "con5", "s40", "t01", "con4", "sg3.mid", "sg1.mid", "tot", "t22", "t23", "t20", "t21",
+    "sg0.mid", "gu5.mid", "t10", "gu4.mid", "t00", "tot2", "sg2.mid", "t52", "t51", "t42", "t43", "t41", "t53", "res",
+    "hid0", "t30", "hid1", "sg5.mid", "hid3", "sg4.mid", "resp", "sc0", "t50", "sc5", "sc2", "sc4", "sc1", "sc3",
+    "hid2", "go0", "go1", "po02", "po12", "hid5", "t40", "hid4", "po03", "gg2.mid", "po01", "gg5.mid", "po10", "po11",
+    "gg0.mid", "po00", "po13", "gg1.mid", "gg4.mid", "zo0.mid", "gg3.mid", "zo1.mid", "gs5", "gs2", "gs0", "gs1",
+    "gs4", "gs3", "gi1", "gi0", "gj0", "gj1", "pi12", "pi02", "pi11", "pi13", "zi1.mid", "zo1.fin", "pi03", "pi01",
+    "zi0.mid", "pi00", "zo0.fin", "pi10", "zi1.fin", "zi0.fin", "colo", "coli",
 ]
 
 
@@ -178,10 +178,12 @@
     for j in range(4):
         cols = pl.ds(pl.multiple_of(1024 * j + x * B, B), B)
         own2.append(pltpu.make_async_copy(w_out.at[:, :, cols], w2.at[j, x], local.at[5 + j]))
-    gift1 = pltpu.make_async_copy(w_in.at[z, :, c], give1, local.at[9])
+    gift1 = pltpu.make_async_copy(w_in.at[z, :, c], give1.at[0], local.at[9])
+    over = lax.rem(z + 2, 4)
+    gift3 = pltpu.make_async_copy(w_in.at[over, :, c], give1.at[1], local.at[21])
     gift2 = pltpu.make_async_copy(w_out.at[c, :, pl.ds(pl.multiple_of(z * 1024, 1024), 1024)], give2, local.at[10])
     scalar = pltpu.make_async_copy(initial_in, initial, local.at[11])
-    for copy in [gift1] + fetch + [gift2] + own1 + own2 + [scalar]:
+    for copy in [gift1, gift3] + fetch + [gift2] + own1 + own2 + [scalar]:
         copy.start()
 
     net = Net(send, recv)
@@ -212,16 +214,21 @@
     ws, wz, wd = {}, {}, {}
     for m in (1, 2):
         for k, i in enumerate(others):
-            src = give1.at[i] if m == 1 else give2.at[:, place(i, B)]
+            src = give1.at[0, i] if m == 1 else give2.at[:, place(i, B)]
             ws[m, k] = net.copy(src, piece(m, x, z), {"x": i})
         for k, i in enumerate(froms):
-            wz[m, k] = Gather(net, "z", quarter(m, i), four)
+            if m == 2:
+                wz[m, k] = Gather(net, "z", quarter(m, i), four)
             slot = net.slots(1)[0]
             for t in range(4):
                 mine = piece(m, i, lax.rem(z + t, 4))
                 wd[m, k, t] = net.copy(mine, mine, {"c": 1 - c}, slot)
             whole = w1.at[i, :, c] if m == 1 else w2.at[:, i, c]
             wd[m, k] = (whole, whole, {"c": 1 - c}, slot)
+
+    wr = [net.copy(give1.at[1, i], piece(1, x, over), {"x": i}) for i in others]
+    up, down = lax.rem(z + 1, 4), lax.rem(z + 3, 4)
+    wn = [[net.copy(piece(1, i, z), piece(1, i, z), {"z": to}) for to in (up, down)] for i in froms]
 
     def scatter(axis, k, slots=None):
         return Scatter(net, axis, sent.at[k], far.at[k], near.at[k], held.at[k], slots)
@@ -263,6 +270,9 @@
     gift1.wait()
     for k in (1, 0, 2):
         net.start(ws[1, k])
+    gift3.wait()
+    for k in (0, 2, 1):
+        net.start(wr[k])
     fetch[0].wait()
     state = start[...]
     for n in range(STEPS):
@@ -474,19 +484,32 @@
 
     def weights_in(m, k):
         net.arrived(ws[m, k])
-        wz[m, k].start()
+        if m == 1:
+            for copy in wn[k]:
+                net.start(copy)
+        else:
+            wz[m, k].start()
         net.start(wd[m, k, 0])
 
+    def straight_in(k):
+        net.arrived(wr[k])
+        net.start(wd[1, k, 2])
+
     def weights_out(m, k):
-        wz[m, k].finish()
-        for t in (1, 3, 2):
-            net.start(wd[m, k, t])
+        if m == 1:
+            for t, copy in ((3, wn[k][0]), (1, wn[k][1])):
+                net.arrived(copy)
+                net.start(wd[m, k, t])
+        else:
+            wz[m, k].finish()
+            for t in (1, 3, 2):
+                net.start(wd[m, k, t])
 
     tasks = {"tot": totals_y, "tot2": totals_x, "res": residuals, "resp": partner_residuals}
     for m in (1, 2):
         for k in range(3):
             tasks[f"w{m}a{k}"] = lambda m=m, k=k: weights_in(m, k)
-            tasks[f"w{m}b{k}"] = wz[m, k].mid
+            tasks[f"w{m}b{k}"] = (lambda k=k: straight_in(k)) if m == 1 else wz[m, k].mid
             tasks[f"w{m}c{k}"] = lambda m=m, k=k: weights_out(m, k)
     for n in range(CHAINS):
         for k in range(4):
@@ -565,12 +588,12 @@
             pltpu.VMEM((B, 128), f32),
             pltpu.VMEM((2, 8, B), f32),
             pltpu.VMEM((2, B, 128), f32),
-            pltpu.VMEM((4, H, B), bf16),
+            pltpu.VMEM((2, 4, H, B), bf16),
             pltpu.VMEM((H, 4 * B), bf16),
             pltpu.SMEM((1,), f32),
             pltpu.SemaphoreType.DMA((LEAVING + 8,)),
             pltpu.SemaphoreType.DMA((ARRIVALS + 8,)),
-            pltpu.SemaphoreType.DMA((21,)),
+            pltpu.SemaphoreType.DMA((22,)),
         ],
         compiler_params=pltpu.CompilerParams(collective_id=0, has_side_effects=True, vmem_limit_bytes=66000000),
     )(start, increments, w_in.reshape(4, 4, 2, H, B), w_out.reshape(2, H, D), initial.reshape(1))

time: 113 us -> 109 us (0.965)
  Pallas kernels: 112 us -> 107 us
    pallas_call x1, Pallas kernels: 110 us -> 105 us  [on_device(): pl.pallas_call(kernel, out_shape=(jax.ShapeDtypeStruct((8, B), f32), jax....]
where the time goes in v6:
time: 109 us; the launch traced here: 108 us
  Pallas kernels  107 us (98%)
  between operations  1.29 us (1%)
    pallas_call x1, Pallas kernels, on_device(): pl.pallas_call(kernel, out_shape=(jax.ShapeDtypeStruct((8, B), f32), jax....  105 us

profile of v6, /device:TPU:1, one launch (start us, length us, event | category | flops | bytes accessed | tf_op | source)
XLA Modules:
  0.0 108.5 jit_solution(814476925347760186)
XLA Ops:
  1.3 105.0 %shard_map.76 = (f32[8,256]{1,0:T(8,128)}, bf16[2,2,256,256]{3,2,1,0:T(8,128)(2,1)}) custom-call(f32[256,256]{1,0:T(8,128)} %start_in.1, f32[3,256,256]{2,1,0:T(8,128)} %inc_in.1, bf16[4,4,2,128,256]{4,3,2,1,0:T(8,128)(2,1)} %bitcast.4, bf16[2,128,4096]{2,1,0:T(8,128)(2,1)} %bitcast.5, f32[1]{0:T(128)} %bitcast.3.initial_in), custom_call_target="tpu_custom_call" | custom-call | tf_op jit(solution)/shard_map/pallas_call | solution.py:560
  106.3 2.2 %shard_map.77 = (f32[256]{0:T(256)}, f32[512,256]{1,0:T(8,128)}, f32[256,512]{1,0:T(8,128)}) custom-call(f32[8,256]{1,0:T(8,128)} %get-tuple-element.5.row, bf16[2,2,256,256]{3,2,1,0:T(8,128)(2,1)} %get-tuple-element.6.blocks), custom_call_target="tpu_custom_call" | custom-call | tf_op jit(solution)/shard_map/pallas_call | solution.py:600

commit v7 on v6

--- a/solution.py
+++ b/solution.py
@@ -23,8 +23,8 @@
 lam_coef = 50.0
 noise_coef = math.sqrt(2.0)
 zscale = 2.0 / math.sqrt(D)
-ARRIVALS = 170
-LEAVING = 48
+ARRIVALS = 141
+LEAVING = 40
 
 
 def place(pos, extent):
@@ -146,8 +146,8 @@
     "hid0", "t30", "hid1", "sg5.mid", "hid3", "sg4.mid", "resp", "sc0", "t50", "sc5", "sc2", "sc4", "sc1", "sc3",
     "hid2", "go0", "go1", "po02", "po12", "hid5", "t40", "hid4", "po03", "gg2.mid", "po01", "gg5.mid", "po10", "po11",
     "gg0.mid", "po00", "po13", "gg1.mid", "gg4.mid", "zo0.mid", "gg3.mid", "zo1.mid", "gs5", "gs2", "gs0", "gs1",
-    "gs4", "gs3", "gi1", "gi0", "gj0", "gj1", "pi12", "pi02", "pi11", "pi13", "zi1.mid", "zo1.fin", "pi03", "pi01",
-    "zi0.mid", "pi00", "zo0.fin", "pi10", "zi1.fin", "zi0.fin", "colo", "coli",
+    "gs4", "gs3", "gi1", "gi0", "gj0", "gj1", "pi12", "pi02", "pi11", "pi13", "pi03", "pi01", "pi10", "pi00",
+    "zi1.mid", "zo1.fin", "zi0.mid", "zo0.fin", "zi1.fin", "zi0.fin", "colo", "coli",
 ]
 
 

time: 109 us -> 108 us (level)
  no operation moved by 1% of the time
where the time goes in v7:
time: 108 us
  Pallas kernels  107 us (99%)
  between operations  1.29 us (1%)
    pallas_call x1, Pallas kernels, on_device(): pl.pallas_call(kernel, out_shape=(jax.ShapeDtypeStruct((8, B), f32), jax....  105 us
    pallas_call x1, Pallas kernels, on_device(): pl.pallas_call(placing, out_shape=(jax.ShapeDtypeStruct((B,), f32), jax.S...  2.16 us

profile of v7, /device:TPU:1, one launch (start us, length us, event | category | flops | bytes accessed | tf_op | source)
XLA Modules:
  0.0 108.1 jit_solution(2558154559813762928)
XLA Ops:
  1.3 104.7 %shard_map.76 = (f32[8,256]{1,0:T(8,128)}, bf16[2,2,256,256]{3,2,1,0:T(8,128)(2,1)}) custom-call(f32[256,256]{1,0:T(8,128)} %start_in.1, f32[3,256,256]{2,1,0:T(8,128)} %inc_in.1, bf16[4,4,2,128,256]{4,3,2,1,0:T(8,128)(2,1)} %bitcast.4, bf16[2,128,4096]{2,1,0:T(8,128)(2,1)} %bitcast.5, f32[1]{0:T(128)} %bitcast.3.initial_in), custom_call_target="tpu_custom_call" | custom-call | tf_op jit(solution)/shard_map/pallas_call | solution.py:560
  106.0 2.2 %shard_map.77 = (f32[256]{0:T(256)}, f32[512,256]{1,0:T(8,128)}, f32[256,512]{1,0:T(8,128)}) custom-call(f32[8,256]{1,0:T(8,128)} %get-tuple-element.5.row, bf16[2,2,256,256]{3,2,1,0:T(8,128)(2,1)} %get-tuple-element.6.blocks), custom_call_target="tpu_custom_call" | custom-call | tf_op jit(solution)/shard_map/pallas_call | solution.py:600
